TPU v7x, 32 devices: a whole 2x2x4 slice. The times are simulated.
32 devices in a mesh: gx: 4 (over x, core), gy: 8 (over z, y).
Axes of the slice: x: 2, y: 2, z: 4, core: 2. Of those that a mesh axis runs over, the one named last changes fastest.
Arguments:
- log_crit: float32 [512, 512, 128], P('gx', 'gy'), may hold values from -4 to 4
- col_bins: int32 [512, 512, 4], P('gx', 'gy'), may hold values from 0 to 127
- rate_table: bfloat16 [128, 64], replicated, may hold values from 0.0039978027 to 0.059814453
- tile_mask: int32 [16, 16, 4], P('gx', 'gy'), may hold values from 0 to 1, as said below
- tile_route: int32 [16, 16, 4], P('gx', 'gy'), may hold values from 0 to 7, as said below
- filt_x: float32 [512], replicated, may hold values from 0.1 to 1, as said below
- filt_y: float32 [512], replicated, may hold values from 0.1 to 1, as said below
Outputs:
- recomb: float32 [512, 512, 128], P('gx', 'gy')
- smoothed: float32 [512, 512, 128], P('gx', 'gy')
- load: float32 [4, 8], P('gx', 'gy')
Inputs may be any that keep to these rules, and one draw needn't show every extreme that they name: `tile_mask`: tiles form blocks of 4 x 2 x 4 (indices a // 4, b // 2); among the blocks with the same a // 4, some block has all 32 tiles active. `tile_route`: counting only tiles with tile_mask 1: among the blocks with the same a // 4 at most 16 active tiles share a route, and in every draw some such row of blocks gives every route exactly 16; at most 4 active tiles of one block share a route, and in every draw some block has 4 that do. filt_x[m] == filt_x[512 - m] for 0 < m < 512. filt_y[n] == filt_y[512 - n] for 0 < n < 512.
All inputs are finite; a program needn't handle non-finite values.
Results may differ from a plain program's by a relative error of at most 0.0003.
Values sent between devices are 32-bit elements; how exact they have to be, the bound alone decides.
No kernel may reach another device: no remote copies, remote signals or barrier semaphores. Data moves between devices by JAX's collectives and lax.ppermute only.
A program may use at most 128 MiB of HBM per device.

v0:
```python
import math

import jax
import jax.numpy as jnp
from jax import lax
from jax.sharding import PartitionSpec as P

steepness = 3.0


def evaluate(field_rows, bin_rows, rate_table):
    tile_count, tile_cells = field_rows.shape
    columns = bin_rows.shape[1]
    z_depth = tile_cells // columns
    bins_total, nodes_total = rate_table.shape
    node_grid = -2.5 + 5.0 * jnp.arange(nodes_total, dtype=jnp.float32) / (nodes_total - 1)
    levels = jnp.arange(bins_total, dtype=jnp.int32)

    def pair_value(operands):
        pair_field, pair_bins = operands
        onehot = (pair_bins.reshape(-1)[:, None] == levels[None, :]).astype(jnp.bfloat16)
        table_rows = jnp.dot(onehot, rate_table, preferred_element_type=jnp.float32).reshape(
            2, columns, 1, nodes_total
        )
        cutoff = jax.nn.sigmoid(
            (pair_field.reshape(2, columns, z_depth, 1) - node_grid) * steepness
        )
        return jnp.sum(cutoff * table_rows, axis=-1).reshape(2, tile_cells)

    values = lax.map(
        pair_value,
        (
            field_rows.reshape(tile_count // 2, 2, tile_cells),
            bin_rows.reshape(tile_count // 2, 2, columns),
        ),
    )
    return values.reshape(tile_count, tile_cells)


def dft_table(length, gain):
    half = length // 2
    indices = jnp.arange(length, dtype=jnp.int32)
    freq = jnp.concatenate(
        [jnp.arange(half + 1, dtype=jnp.int32), jnp.arange(1, half, dtype=jnp.int32)]
    )
    angles = (
        2.0 * math.pi / length * (indices[:, None] * freq[None, :] % length).astype(jnp.float32)
    )
    is_cosine = indices[None, :] < half + 1
    table = jnp.where(is_cosine, jnp.cos(angles), jnp.sin(angles))
    weight = jnp.concatenate([gain[: half + 1], gain[1:half]])
    doubled = jnp.where((freq == 0) | (freq == half), 1.0, 2.0).astype(jnp.float32)
    return (table, weight * doubled / length)


def smooth_plane(pencil, filt_x, filt_y):
    z_local, size_x, size_y = pencil.shape
    table_y, weight_y = dft_table(size_y, filt_y)
    spectrum = (
        jnp.dot(pencil.reshape(-1, size_y), table_y, precision=lax.Precision.HIGHEST) * weight_y
    )
    along_y = jnp.dot(spectrum, table_y.T, precision=lax.Precision.HIGHEST).reshape(
        z_local, size_x, size_y
    )
    table_x, weight_x = dft_table(size_x, filt_x)
    spectrum_x = (
        jnp.einsum("zxy,xk->zky", along_y, table_x, precision=lax.Precision.HIGHEST)
        * weight_x[None, :, None]
    )
    return jnp.einsum("zky,xk->zxy", spectrum_x, table_x, precision=lax.Precision.HIGHEST)


def on_device(log_crit, col_bins, rate_table, tile_mask, tile_route, filt_x, filt_y):
    blocks_x, blocks_y, blocks_z = tile_mask.shape
    cells_x, cells_y, depth_all = log_crit.shape
    tile_edge = cells_x // blocks_x
    tile_count = blocks_x * blocks_y * blocks_z
    tile_cells = tile_edge * tile_edge * tile_edge
    tile_data = (
        log_crit.reshape(blocks_x, tile_edge, blocks_y, tile_edge, blocks_z, tile_edge)
        .transpose(0, 2, 4, 1, 3, 5)
        .reshape(tile_count, tile_cells)
    )
    tile_bins = (
        col_bins.reshape(blocks_x, tile_edge, blocks_y, tile_edge, blocks_z)
        .transpose(0, 2, 4, 1, 3)
        .reshape(tile_count, tile_edge * tile_edge)
    )
    is_active = tile_mask.reshape(tile_count)
    target = tile_route.reshape(tile_count)
    receivers = lax.axis_size("gy")
    span_x = lax.axis_size("gx")
    capacity = tile_count // 2
    recomb_tiles = evaluate(tile_data, tile_bins, rate_table)
    recomb_tiles = jnp.where(is_active[:, None] == 1, recomb_tiles, 0.0)
    tile_means = jnp.mean(recomb_tiles, axis=1)
    route_ids = jnp.arange(receivers, dtype=jnp.int32)
    contribution = (
        jnp.sum(jnp.where(target[:, None] == route_ids[None, :], tile_means[:, None], 0.0), axis=0)
        / capacity
    )
    device_load = lax.psum_scatter(contribution, "gy", scatter_dimension=0, tiled=True)[0]
    recomb = (
        recomb_tiles.reshape(blocks_x, blocks_y, blocks_z, tile_edge, tile_edge, tile_edge)
        .transpose(0, 3, 1, 4, 2, 5)
        .reshape(cells_x, cells_y, depth_all)
    )
    z_first = recomb.transpose(2, 0, 1)
    pencil = lax.all_to_all(
        lax.all_to_all(z_first, "gx", split_axis=0, concat_axis=1, tiled=True),
        "gy",
        split_axis=0,
        concat_axis=2,
        tiled=True,
    )
    smoothed_pencil = smooth_plane(pencil, filt_x, filt_y)
    returned_pencil = lax.all_to_all(
        lax.all_to_all(smoothed_pencil, "gx", split_axis=1, concat_axis=0, tiled=True),
        "gy",
        split_axis=2,
        concat_axis=0,
        tiled=True,
    )
    z_local = depth_all // (span_x * receivers)
    smoothed = (
        returned_pencil.reshape(receivers, span_x, z_local, cells_x, cells_y)
        .transpose(3, 4, 1, 0, 2)
        .reshape(cells_x, cells_y, depth_all)
    )
    return (recomb, smoothed, device_load.reshape(1, 1))


def solution(mesh):
    placed = (
        P("gx", "gy", None),
        P("gx", "gy", None),
        P(),
        P("gx", "gy", None),
        P("gx", "gy", None),
        P(),
        P(),
    )
    return jax.shard_map(
        on_device,
        mesh=mesh,
        in_specs=placed,
        out_specs=(P("gx", "gy", None), P("gx", "gy", None), P("gx", "gy")),
        check_vma=False,
    )
```

profile of v0, /device:TPU:8, one launch (start us, length us, event | category | flops | bytes accessed | tf_op | source)
XLA Modules:
  0.0 667.1 jit_solution(11711818687086749989)
XLA Ops:
  0.6 12.9 %reshape.155 = f32[4,32,2,32,4,32]{5,4,3,2,1,0:T(4,128)} reshape(f32[128,64,128]{2,1,0:T(8,128)} %param.9) | data formatting | bytes 8388608 | tf_op jit(solution)/shard_map/reshape | solution.py:80
  13.6 12.6 %copy.91 = f32[4,32,2,32,4,32]{5,3,1,4,2,0:T(8,128)} copy(f32[4,32,2,32,4,32]{5,4,3,2,1,0:T(4,128)} %reshape.155) | data formatting | bytes 8388608 | tf_op jit(solution)/shard_map/reshape | solution.py:80
  26.2 16.7 %reshape_reshape.6 = f32[16,2,32768]{2,1,0:T(2,128)} reshape(f32[4,2,4,32,32,32]{5,4,3,2,1,0:T(8,128)} %bitcast.85) | data formatting | bytes 8388608 | tf_op jit(solution)/shard_map/reshape;reshape | solution.py:33
  43.8 162.5 %while.12 = (s32[]{:T(128)}, f32[16,2,32768]{2,1,0:T(2,128)}, f32[16,2,32768]{2,1,0:T(2,128)}, s32[16,2,1024]{2,1,0:T(2,128)S(1)}, bf16[128,64]{0,1:T(8,128)(2,1)S(1)}) while((s32[]{:T(128)}, f32[16,2,32768]{2,1,0:T(2,128)}, f32[16,2,32768]{2,1,0:T(2,128)}, s32[16,2,1024]{2,1,0:T(2,128)S(1)}, ...), condition=%wide.region_2.3_spmd.clone.clone, body=%wide.region_0.2_spmd.clone.sunk.clone | while | flops 63111296 | bytes 5825105 | solution.py:30
  44.6 1.0 constant_dynamic-slice_fusion.3
  46.4 6.0 multiply_reduce_fusion.3
  56.5 6.0 multiply_reduce_fusion.3
  66.7 6.0 multiply_reduce_fusion.3
  76.8 6.0 multiply_reduce_fusion.3
  87.0 6.0 multiply_reduce_fusion.3
  97.1 6.0 multiply_reduce_fusion.3
  107.3 6.0 multiply_reduce_fusion.3
  117.5 6.0 multiply_reduce_fusion.3
  127.6 6.0 multiply_reduce_fusion.3
  137.8 6.0 multiply_reduce_fusion.3
  147.9 6.0 multiply_reduce_fusion.3
  158.1 6.0 multiply_reduce_fusion.3
  168.2 6.0 multiply_reduce_fusion.3
  178.4 6.0 multiply_reduce_fusion.3
  188.6 6.0 multiply_reduce_fusion.3
  198.7 6.0 multiply_reduce_fusion.3
  206.3 15.3 %reshape.157 = f32[4,2,4,32,32,32]{5,4,3,2,1,0:T(8,128)} reshape(f32[16,2,32768]{2,1,0:T(2,128)} %get-tuple-element.40) | data formatting | bytes 8388608 | tf_op jit(solution)/shard_map/reshape | solution.py:37
  221.6 21.9 %copy.65 = f32[4,2,4,32,32,32]{3,0,4,1,5,2:T(4,128)} copy(f32[4,2,4,32,32,32]{5,4,3,2,1,0:T(8,128)} %reshape.157) | data formatting | bytes 8388608 | tf_op jit(solution)/shard_map/reshape | solution.py:37
  243.7 16.4 %select_bitcast_fusion = f32[4,32,2,32,4,32]{1,0,3,2,5,4:T(4,128)} fusion(f32[4,2,4,32,32,32]{3,0,4,1,5,2:T(4,128)} %copy.65, pred[4,2,4]{0,1,2:T(4,128)(4,1)S(1)} %copy.62), kind=kLoop, calls=%fused_computation.13 | loop fusion | flops 1048576 | bytes 8388640 | tf_op jit(solution)/shard_map/transpose | solution.py:105
  260.1 13.5 %reshape.158 = f32[128,64,128]{0,1,2:T(8,128)} reshape(f32[4,32,2,32,4,32]{1,0,3,2,5,4:T(4,128)} %select_bitcast_fusion) | data formatting | bytes 8388608 | tf_op jit(solution)/shard_map/reshape | solution.py:106
  273.5 51.9 %all_to_all.66 = f32[128,128,64]{1,2,0:T(8,128)S(1)} all-to-all(f32[128,128,64]{1,2,0:T(8,128)} %bitcast.87), channel_id=1, replica_groups=mesh['gx'=4,'gy'=8] {'gx'}, dimensions={0} | all-to-all | bytes 8388608 | tf_op jit(solution)/shard_map/all_to_all | solution.py:110
  325.4 2.6 copy.92
  328.0 6.6 all-to-all-start.1
  335.0 89.8 %all-to-all-done.1 = f32[32,512,64]{1,2,0:T(8,128)} async-done(((f32[32,512,64]{1,2,0:T(8,128)}), f32[32,512,64]{1,2,0:T(8,128)}, u32[]{:S(2)}, u32[]{:S(2)}) %all-to-all-start.1) | async-done | bytes 4194336 | tf_op jit(solution)/shard_map/all_to_all | solution.py:109
  424.8 4.9 copy.67
  429.6 2.0 copy.84
  431.6 11.4 %fusion.25 = f32[2048,512]{1,0:T(8,128)S(1)} fusion(f32[2048,512]{0,1:T(8,128)S(1)} %bitcast.88, s32[512]{0:T(512)S(1)} %get-tuple-element.78, pred[512]{0:T(512)(128)(4,1)S(1)} %iota_compare_fusion.3), kind=kOutput, calls=%fused_computation.37 | convolution fusion | flops 6446383104 | bytes 8391168 | tf_op jit(solution)/shard_map/dot_general | solution.py:60
  443.0 11.2 %fusion.9 = f32[2048,512]{1,0:T(8,128)S(1)} fusion(f32[2048,512]{1,0:T(8,128)S(1)} %fusion.25, f32[512]{0:T(512)S(1)} %fusion.26, s32[512]{0:T(512)S(1)} %get-tuple-element.78, pred[512]{0:T(512)(128)(4,1)S(1)} %iota_compare_fusion.3), kind=kOutput, calls=%fused_computation.19 | convolution fusion | flops 6447431680 | bytes 8393216 | tf_op jit(solution)/shard_map/dot_general | solution.py:62
  454.2 11.8 %fusion.19 = f32[512,4,512]{2,0,1:T(8,128)S(1)} fusion(f32[4,512,512]{2,1,0:T(8,128)S(1)} %bitcast.97, s32[512]{0:T(512)S(1)} %get-tuple-element.78, pred[512]{0:T(512)(128)(4,1)S(1)} %iota_compare_fusion.3), kind=kOutput, calls=%fused_computation.30 | convolution fusion | flops 6446383104 | bytes 8391168 | tf_op jit(solution)/shard_map/zxy,xk->zky/dot_general | solution.py:67
  466.0 11.8 %fusion.11 = f32[4,512,512]{2,1,0:T(8,128)S(1)} fusion(f32[512,4,512]{2,0,1:T(8,128)S(1)} %fusion.19, f32[512]{0:T(512)S(1)} %get-tuple-element.76, s32[512]{0:T(512)S(1)} %get-tuple-element.78, pred[512]{0:T(512)(128)(4,1)S(1)} %iota_compare_fusion.3), kind=kOutput, calls=%fused_computation.21 | convolution fusion | flops 6447431680 | bytes 8393216 | tf_op jit(solution)/shard_map/zky,xk->zxy/dot_general | solution.py:70
  477.8 2.7 copy.69
  480.5 50.7 %all_to_all.67 = f32[4,512,512]{2,0,1:T(4,128)S(1)} all-to-all(f32[4,512,512]{2,0,1:T(4,128)S(1)} %copy.69), channel_id=1, replica_groups=mesh['gx'=4,'gy'=8] {'gx'}, dimensions={1} | all-to-all | bytes 8388608 | tf_op jit(solution)/shard_map/all_to_all | solution.py:118
  531.2 1.3 copy.70
  532.6 2.7 copy.71
  535.3 5.4 copy.72
  540.7 7.0 %all-to-all-start.3 = ((f32[16,128,512]{1,0,2:T(8,128)}), f32[16,128,512]{1,0,2:T(8,128)}, u32[]{:S(2)}, u32[]{:S(2)}) async-start(f32[16,128,512]{1,0,2:T(8,128)} %copy.72), calls=%async_computation.3 | async-start | bytes 8388608 | tf_op jit(solution)/shard_map/all_to_all | solution.py:117
  547.8 4.1 select_reduce_fusion
  552.2 96.5 %all-reduce = f32[8]{0:T(128)S(1)} all-reduce(f32[8]{0:T(128)S(1)} %broadcast_multiply_fusion.1), channel_id=2, replica_groups=mesh['gx'=4,'gy'=8] {'gy'}, use_global_device_ids=true, to_apply=%region_5.6.clone | all-reduce | flops 8 | bytes 64
  648.7 5.4 copy.76
  654.7 1.2 dynamic-slice.1
  655.9 3.4 copy.74
  659.3 2.2 copy.75
  661.6 5.4 copy.77
  (210 shorter events, 67.7 us)
Async XLA Ops:
  26.2 16.7 %copy-start.1 = (s32[128,64,4]{0,2,1:T(4,128)S(1)}, s32[128,64,4]{0,2,1:T(4,128)}, u32[]{:S(2)}) copy-start(s32[128,64,4]{0,2,1:T(4,128)} %param.10) | copy-start | bytes 393220
  26.2 17.6 %copy-start = (bf16[128,64]{0,1:T(8,128)(2,1)S(1)}, bf16[128,64]{0,1:T(8,128)(2,1)}, u32[]{:S(2)}) copy-start(bf16[128,64]{0,1:T(8,128)(2,1)} %param.11) | copy-start | bytes 49156
  221.6 21.9 %copy-start.4 = (s32[4,2,4]{2,1,0:T(2,128)S(1)}, s32[4,2,4]{2,1,0:T(2,128)}, u32[]{:S(2)}) copy-start(s32[4,2,4]{2,1,0:T(2,128)} %param.12) | copy-start | bytes 388
  328.0 6.7 copy-start.2
  328.0 6.7 %copy-start.3 = (f32[512]{0:T(512)S(1)}, f32[512]{0:T(512)}, u32[]{:S(2)}) copy-start(f32[512]{0:T(512)} %param.15) | copy-start | bytes 6148
  328.0 96.8 %all-to-all-start.1 = ((f32[32,512,64]{1,2,0:T(8,128)}), f32[32,512,64]{1,2,0:T(8,128)}, u32[]{:S(2)}, u32[]{:S(2)}) async-start(f32[32,512,64]{1,2,0:T(8,128)} %bitcast.89), calls=%async_computation.1 | async-start | bytes 8388608 | tf_op jit(solution)/shard_map/all_to_all | solution.py:109
  540.7 115.2 %all-to-all-start.3 = ((f32[16,128,512]{1,0,2:T(8,128)}), f32[16,128,512]{1,0,2:T(8,128)}, u32[]{:S(2)}, u32[]{:S(2)}) async-start(f32[16,128,512]{1,0,2:T(8,128)} %copy.72), calls=%async_computation.3 | async-start | bytes 8388608 | tf_op jit(solution)/shard_map/all_to_all | solution.py:117
  547.7 4.3 copy-start.5
  648.7 5.4 copy-start.6
where the time goes:
time: 678 us; the launch traced here: 667 us
  blocking collectives  199 us (29%)
  local copies, waits for them, and re-layouts  189 us (28%)
  other arithmetic  116 us (17%)
  waiting for transfers between devices  89.8 us (13%)
  matrix products  57.8 us (9%)
  starting transfers between devices  13.6 us (2%)
    unnamed x1, blocking collectives  96.5 us
    reduce_sum x16, other arithmetic, pair_value(): return jnp.sum(cutoff * table_rows, axis=-1).reshape(2, tile_cells)  95.3 us
    all_to_all x1, waiting for transfers between devices, on_device(): lax.all_to_all(lax.all_to_all(z_first, 'gx', split_axis=0, concat_axis=1,...  89.8 us
    all_to_all x1, blocking collectives, on_device(): lax.all_to_all(z_first, 'gx', split_axis=0, concat_axis=1, tiled=True)  51.9 us
    all_to_all x1, blocking collectives, on_device(): lax.all_to_all(smoothed_pencil, 'gx', split_axis=1, concat_axis=0, tiled=...  50.7 us
    reshape x2, local copies, waits for them, and re-layouts, evaluate(): return values.reshape(tile_count, tile_cells)  37.2 us
    reshape x2, local copies, waits for them, and re-layouts, on_device(): log_crit.reshape(blocks_x, tile_edge, blocks_y, tile_edge, blocks_z, tile...  25.6 us
    another operation x1, local copies, waits for them, and re-layouts, evaluate(): field_rows.reshape(tile_count // 2, 2, tile_cells)  16.7 us
  transfers between devices with their start and end apart: 2, of which 1 were waited for; matrix products, arithmetic and copies ran while one was open for 2% of the time, Pallas kernels for 0%

commit v1 on v0

v1 whole, which is shorter than its diff:
```python
import functools

import jax
import jax.numpy as jnp
import numpy as np
from jax import lax
from jax.experimental import pallas as pl
from jax.experimental.pallas import tpu as pltpu
from jax.sharding import PartitionSpec as P

STEEPNESS = 3.0
ROWS = 8
VMEM_BYTES = 40 * 1024 * 1024


def node_grid(nodes):
    return np.float32(-2.5) + np.float32(5.0) * np.arange(nodes, dtype=np.float32) / np.float32(nodes - 1)


def evaluate_kernel(run_first, runs, edge, devices, mask_ref, field_ref, bins_ref, rate_ref, cells_ref, sums_ref, row_scratch, field_scratch):
    step = pl.program_id(0)
    size_x, rows, size_z = field_ref.shape
    nodes, levels = rate_ref.shape
    planes = cells_ref.shape[1]
    half_nodes = np.float32(0.5 * STEEPNESS) * node_grid(nodes)
    tile_b = step * rows // edge
    tiles_x = size_x // edge
    lane = lax.broadcasted_iota(jnp.int32, (1, size_x), 1)
    level = lax.broadcasted_iota(jnp.int32, (levels, size_x), 0)
    field = field_ref.reshape(size_x * rows, size_z)
    cells = cells_ref.reshape(devices * planes * rows, size_x)

    @pl.when(step % (edge // rows) == 0)
    def _():
        sums_ref[...] = jnp.zeros_like(sums_ref)

    for run in range(runs):
        active = jnp.zeros((1, size_x), jnp.float32)
        for a in range(tiles_x):
            flag = mask_ref[a, tile_b, run_first + run]
            here = (lane >= a * edge) & (lane < (a + 1) * edge)
            active = jnp.where(here & (flag == 1), 0.5, active)
        for y in range(rows):
            onehot = (level == bins_ref[y, pl.ds(run_first + run, 1), :]).astype(jnp.bfloat16)
            row_scratch[run, y] = jnp.dot(rate_ref[...], onehot, preferred_element_type=jnp.float32) * active

    def one_row(y, carry):
        turned = field[pl.ds(y, size_x, stride=rows), :].T
        scaled = (turned * (0.5 * STEEPNESS))[run_first * edge : (run_first + runs) * edge]
        for run in range(runs):
            values = scaled[run * edge : (run + 1) * edge]
            total = jnp.broadcast_to(jnp.sum(row_scratch[run, y], axis=0, keepdims=True), values.shape)
            for q in range(nodes):
                rate = row_scratch[run, y, pl.ds(q, 1), :]
                total = total + rate * jnp.tanh(values - half_nodes[q])
            plane, first = divmod(run * edge, devices)
            cells[pl.ds(first * planes * rows + plane * rows + y, edge, stride=planes * rows), :] = total
            part = total[0:8]
            for k in range(8, edge, 8):
                part = part + total[k : k + 8]
            sums_ref[0, run] += part
        return carry

    lax.fori_loop(0, rows, one_row, 0)


def evaluate(log_crit, bins, rates, tile_mask, run_first, runs, devices):
    size_x, size_y, size_z = log_crit.shape
    edge = size_x // tile_mask.shape[0]
    planes = runs * edge // devices
    tiles_y = tile_mask.shape[1]
    nodes, levels = rates.shape
    steps = size_y // ROWS
    return pl.pallas_call(
        functools.partial(evaluate_kernel, run_first, runs, edge, devices),
        grid=(steps,),
        in_specs=[
            pl.BlockSpec(memory_space=pltpu.SMEM),
            pl.BlockSpec((size_x, ROWS, size_z), lambda j: (0, j, 0)),
            pl.BlockSpec((ROWS, bins.shape[1], size_x), lambda j: (j, 0, 0)),
            pl.BlockSpec((nodes, levels), lambda j: (0, 0)),
        ],
        out_specs=[
            pl.BlockSpec((devices, planes, ROWS, size_x), lambda j: (0, 0, j, 0)),
            pl.BlockSpec((1, runs, 8, size_x), lambda j: (j * ROWS // edge, 0, 0, 0)),
        ],
        out_shape=[
            jax.ShapeDtypeStruct((devices, planes, size_y, size_x), jnp.float32),
            jax.ShapeDtypeStruct((tiles_y, runs, 8, size_x), jnp.float32),
        ],
        scratch_shapes=[
            pltpu.VMEM((runs, ROWS, nodes, size_x), jnp.float32),
            pltpu.VMEM((size_z, size_x), jnp.float32),
        ],
        cost_estimate=pl.CostEstimate(
            flops=runs * edge * size_x * size_y * nodes * 4, bytes_accessed=6 << 20, transcendentals=0
        ),
        compiler_params=pltpu.CompilerParams(vmem_limit_bytes=VMEM_BYTES),
        name="evaluate",
    )(tile_mask, log_crit, bins, rates)


def split(value):
    high = value.astype(jnp.bfloat16)
    low = (value - high.astype(jnp.float32)).astype(jnp.bfloat16)
    return high, low


def product(left, right):
    dot = functools.partial(jnp.dot, preferred_element_type=jnp.float32)
    return dot(left[0], right[0]) + (dot(left[0], right[1]) + dot(left[1], right[0]))


def window_kernel(span_x, span_y, x_ref, y_ref, plane_ref, out_ref):
    rows, lanes = plane_ref.shape[-2:]
    plane = jnp.concatenate(
        [
            jnp.concatenate([plane_ref[i * span_y + j, 0] for i in range(span_x)], axis=1)
            for j in range(span_y)
        ],
        axis=0,
    )
    along_y = product(split(y_ref[...]), split(plane))
    both = product(split(along_y), split(x_ref[...]))
    for i in range(span_x):
        for j in range(span_y):
            out_ref[i * span_y + j, 0] = both[j * rows : (j + 1) * rows, i * lanes : (i + 1) * lanes]


def apply_window(planes, matrix_x, matrix_y, span_x, span_y):
    devices, count, rows, lanes = planes.shape
    size_x, size_y = matrix_x.shape[0], matrix_y.shape[0]
    spec = pl.BlockSpec((devices, 1, rows, lanes), lambda p: (0, p, 0, 0))
    return pl.pallas_call(
        functools.partial(window_kernel, span_x, span_y),
        grid=(count,),
        in_specs=[
            pl.BlockSpec((size_x, size_x), lambda p: (0, 0)),
            pl.BlockSpec((size_y, size_y), lambda p: (0, 0)),
            spec,
        ],
        out_specs=spec,
        out_shape=jax.ShapeDtypeStruct(planes.shape, jnp.float32),
        cost_estimate=pl.CostEstimate(
            flops=count * 6 * size_x * size_y * (size_x + size_y), bytes_accessed=4 << 20, transcendentals=0
        ),
        compiler_params=pltpu.CompilerParams(vmem_limit_bytes=VMEM_BYTES),
        name="window",
    )(matrix_x, matrix_y, planes)


def restore_kernel(edge, count, *refs):
    parts, out_ref = refs[:count], refs[count]
    size_x, rows, size_z = out_ref.shape
    out = out_ref.reshape(size_x * rows, size_z)

    def one_row(y, carry):
        pieces = []
        for part in parts:
            devices, planes = part.shape[:2]
            flat = part.reshape(devices * planes * rows, size_x)
            for plane in range(planes):
                pieces.append(flat[pl.ds(plane * rows + y, devices, stride=planes * rows), :])
        whole = pieces[0] if len(pieces) == 1 else jnp.concatenate(pieces, axis=0)
        out[pl.ds(y, size_x, stride=rows), :] = whole.T
        return carry

    lax.fori_loop(0, rows, one_row, 0)


def restore(parts, edge):
    size_y, size_x = parts[0].shape[2:]
    size_z = sum(part.shape[0] * part.shape[1] for part in parts)
    return pl.pallas_call(
        functools.partial(restore_kernel, edge, len(parts)),
        grid=(size_y // ROWS,),
        in_specs=[
            pl.BlockSpec((*part.shape[:2], ROWS, size_x), lambda j: (0, 0, j, 0)) for part in parts
        ],
        out_specs=pl.BlockSpec((size_x, ROWS, size_z), lambda j: (0, j, 0)),
        out_shape=jax.ShapeDtypeStruct((size_x, size_y, size_z), jnp.float32),
        cost_estimate=pl.CostEstimate(flops=1 << 30, bytes_accessed=8 << 20, transcendentals=0),
        compiler_params=pltpu.CompilerParams(vmem_limit_bytes=VMEM_BYTES),
        name="restore",
    )(*parts)


def wave_table(length):
    half = length // 2
    freq = np.concatenate([np.arange(half + 1), np.arange(1, half)])
    angle = 2.0 * np.pi / length * (np.arange(length)[:, None] * freq[None, :] % length)
    table = np.where(np.arange(length)[None, :] <= half, np.cos(angle), np.sin(angle))
    doubled = np.where((freq == 0) | (freq == half), 1.0, 2.0) / length
    return table.astype(np.float32), doubled.astype(np.float32)


def window_matrix(gain, table, doubled):
    length = gain.shape[0]
    half = length // 2
    weight = jnp.concatenate([gain[: half + 1], gain[1:half]]) * doubled
    return lax.dot_general(
        table * weight[None, :], table, (((1,), (1,)), ((), ())), precision=lax.Precision.HIGHEST
    )


def on_device(groups, log_crit, col_bins, rate_table, tile_mask, tile_route, filt_x, filt_y):
    span_x, span_y = lax.axis_size("gx"), lax.axis_size("gy")
    devices = span_x * span_y
    size_x, size_y, size_z = log_crit.shape
    blocks_x, blocks_y, blocks_z = tile_mask.shape
    edge = size_x // blocks_x
    tile_count = blocks_x * blocks_y * blocks_z
    bins = col_bins.transpose(1, 2, 0)
    rates = rate_table.T
    cells, sums = [], []
    for first, runs in groups:
        part, total = evaluate(log_crit, bins, rates, tile_mask, first, runs, devices)
        cells.append(part)
        sums.append(total)
    tables = {length: wave_table(length) for length in (filt_x.shape[0], filt_y.shape[0])}
    tables = {length: tuple(jnp.asarray(item) for item in pair) for length, pair in tables.items()}
    matrix_x = window_matrix(filt_x, *tables[filt_x.shape[0]])
    matrix_y = window_matrix(filt_y, *tables[filt_y.shape[0]])
    exchange = functools.partial(
        lax.all_to_all, axis_name=("gx", "gy"), split_axis=0, concat_axis=0, tiled=True
    )
    pencils = [exchange(part) for part in cells]
    filtered = [apply_window(part, matrix_x, matrix_y, span_x, span_y) for part in pencils]
    returned = [exchange(part) for part in filtered]
    recomb = restore(cells, edge)
    smoothed = restore(returned, edge)
    tile_sums = jnp.concatenate(sums, axis=1).sum(axis=2)
    tile_means = tile_sums.reshape(blocks_y, blocks_z, blocks_x, edge).sum(axis=3) / (edge * edge * edge)
    route = tile_route.transpose(1, 2, 0)
    workers = jnp.arange(span_y, dtype=jnp.int32)
    shares = jnp.where(route[..., None] == workers, tile_means[..., None], 0.0)
    contribution = shares.sum(axis=(0, 1, 2)) / (tile_count // 2)
    load = lax.psum_scatter(contribution, "gy", scatter_dimension=0, tiled=True)
    return recomb, smoothed, load.reshape(1, 1)


def split_runs(size_z, edge, devices):
    runs = size_z // edge
    smallest = max(1, devices // edge)
    if smallest * 2 > runs:
        return ((0, runs),)
    half = runs // 2
    return ((0, half), (half, runs - half))


def solution(mesh):
    placed = (
        P("gx", "gy", None),
        P("gx", "gy", None),
        P(),
        P("gx", "gy", None),
        P("gx", "gy", None),
        P(),
        P(),
    )
    devices = mesh.shape["gx"] * mesh.shape["gy"]

    def whole(*args):
        size_z = args[0].shape[2]
        edge = args[0].shape[0] // args[3].shape[0]
        groups = split_runs(size_z, edge, devices)
        return jax.shard_map(
            functools.partial(on_device, groups),
            mesh=mesh,
            in_specs=placed,
            out_specs=(P("gx", "gy", None), P("gx", "gy", None), P("gx", "gy")),
            check_vma=False,
        )(*args)

    return whole
```

time: 678 us -> 278 us (0.41); the launches traced: 667 us -> 277 us
  local copies, waits for them, and re-layouts: 189 us -> 13.7 us
  blocking collectives: 199 us -> 56.3 us
  other arithmetic: 116 us -> 0.31 us
  Pallas kernels: 0 us -> 83.4 us
  matrix products: 57.8 us -> 5.34 us
  starting transfers between devices: 13.6 us -> 24.5 us
    all_to_all x2 -> x0, blocking collectives: 103 us -> none  [the longest x1 51.9 us: on_device(): lax.all_to_all(z_first, 'gx', split_axis=0, concat_axis=1, tiled=True)]
    reduce_sum x18 -> x3, other arithmetic: 99.5 us -> 0.22 us  [the longest x1 0.1 us: on_device(): contribution = shares.sum(axis=(0, 1, 2)) / (tile_count // 2)]
    pallas_call x0 -> x6, Pallas kernels: none -> 83.4 us  [the longest x2 55.4 us: evaluate(): pl.pallas_call(functools.partial(evaluate_kernel, run_first, runs, edge,...]
    reshape x7 -> x1, local copies, waits for them, and re-layouts: 76.8 us -> 0.09 us  [on_device(): tile_sums.reshape(blocks_y, blocks_z, blocks_x, edge).sum(axis=3)]
    dot_general x20 -> x2, matrix products: 57.8 us -> 5.34 us  [window_matrix(): lax.dot_general(table * weight[None, :], table, (((1,), (1,)), ((), ())),...]
    unnamed x1, blocking collectives: 96.5 us -> 56.3 us
    all_to_all x6 -> x0, local copies, waits for them, and re-layouts: 20.4 us -> none  [the longest x3 9.5 us: on_device(): lax.all_to_all(smoothed_pencil, 'gx', split_axis=1, concat_axis=0, tiled=...]
    another operation x2 -> x0, local copies, waits for them, and re-layouts: 17 us -> none  [the longest x1 16.7 us: evaluate(): field_rows.reshape(tile_count // 2, 2, tile_cells)]
  transfers between devices with their start and end apart: 2 -> 4, of which waited for: 1 -> 3; matrix products, arithmetic and copies ran while one was open for 2% -> 3% of each run, Pallas kernels for 0% -> 17%
where the time goes in v1:
time: 278 us; the launch traced here: 277 us
  waiting for transfers between devices  92.7 us (33%)
  Pallas kernels  83.4 us (30%)
  blocking collectives  56.3 us (20%)
  starting transfers between devices  24.5 us (9%)
  local copies, waits for them, and re-layouts  13.7 us (5%)
  matrix products  5.34 us (2%)
    unnamed x1, blocking collectives  56.3 us
    pallas_call x2, Pallas kernels, evaluate(): pl.pallas_call(functools.partial(evaluate_kernel, run_first, runs, edge,...  55.4 us
    all_to_all x2, waiting for transfers between devices, on_device(): pencils = [exchange(part) for part in cells]  53.1 us
    all_to_all x2, waiting for transfers between devices, on_device(): returned = [exchange(part) for part in filtered]  39.6 us
    pallas_call x2, Pallas kernels, restore(): pl.pallas_call(functools.partial(restore_kernel, edge, len(parts)), grid=...  19.1 us
    unnamed x38, local copies, waits for them, and re-layouts  13.4 us
    all_to_all x2, starting transfers between devices, on_device(): pencils = [exchange(part) for part in cells]  12.5 us
    all_to_all x2, starting transfers between devices, on_device(): returned = [exchange(part) for part in filtered]  12 us
  transfers between devices with their start and end apart: 4, of which 3 were waited for; matrix products, arithmetic and copies ran while one was open for 3% of the time, Pallas kernels for 17%

profile of v1, /device:TPU:8, one launch (start us, length us, event | category | flops | bytes accessed | tf_op | source)
XLA Modules:
  0.0 277.0 jit_solution(88626113185627163)
XLA Ops:
  0.6 0.0 copy-start
  0.6 2.2 copy-done
  2.8 0.9 copy-done.6
  3.7 0.7 copy-done.8
  4.4 0.7 copy-done.10
  5.1 28.3 %evaluate.3 = (f32[32,2,64,128]{3,2,1,0:T(8,128)}, f32[2,2,8,128]{3,2,1,0:T(8,128)S(1)}) custom-call(s32[4,2,4]{2,1,0:T(2,128)S(1)} %copy-done.10, f32[128,64,128]{2,1,0:T(8,128)S(1)} %copy-done, s32[64,4,128]{2,1,0:T(4,128)S(1)} %bitcast.9, bf16[64,128]{1,0:T(8,128)(2,1)S(1)} %bitcast.11), custom_call_target="tpu_custom_call" | custom-call | flops 134217728 | bytes 6291456 | tf_op jit(solution)/shard_map/evaluate/pallas_call | solution.py:74
  33.4 6.0 %all-to-all-start.2 = ((f32[32,2,64,128]{3,2,1,0:T(8,128)}), f32[32,2,64,128]{3,2,1,0:T(8,128)S(1)}, u32[]{:S(2)}, u32[]{:S(2)}) async-start(f32[32,2,64,128]{3,2,1,0:T(8,128)} %get-tuple-element.8.refs_1_), calls=%async_computation.2 | async-start | bytes 4194304 | tf_op jit(solution)/shard_map/all_to_all | solution.py:227
  39.5 0.0 copy-done.7
  39.5 0.0 copy-done.9
  39.5 0.0 copy-done.11
  39.5 0.0 copy-start.1
  39.5 2.2 copy-done.1
  41.7 27.1 %evaluate.2 = (f32[32,2,64,128]{3,2,1,0:T(8,128)}, f32[2,2,8,128]{3,2,1,0:T(8,128)S(1)}) custom-call(s32[4,2,4]{2,1,0:T(2,128)S(1)} %copy-done.11, f32[128,64,128]{2,1,0:T(8,128)S(1)} %copy-done.1, s32[64,4,128]{2,1,0:T(4,128)S(1)} %bitcast.10, bf16[64,128]{1,0:T(8,128)(2,1)S(1)} %bitcast.12), custom_call_target="tpu_custom_call" | custom-call | flops 134217728 | bytes 6291456 | tf_op jit(solution)/shard_map/evaluate/pallas_call | solution.py:74
  68.8 17.7 %all-to-all-done.2.plane_ref = f32[32,2,64,128]{3,2,1,0:T(8,128)S(1)} async-done(((f32[32,2,64,128]{3,2,1,0:T(8,128)}), f32[32,2,64,128]{3,2,1,0:T(8,128)S(1)}, u32[]{:S(2)}, u32[]{:S(2)}) %all-to-all-start.2) | async-done | bytes 2097184 | tf_op jit(solution)/shard_map/all_to_all | solution.py:227
  86.5 6.5 %all-to-all-start = ((f32[32,2,64,128]{3,2,1,0:T(8,128)}), f32[32,2,64,128]{3,2,1,0:T(8,128)}, u32[]{:S(2)}, u32[]{:S(2)}) async-start(f32[32,2,64,128]{3,2,1,0:T(8,128)} %get-tuple-element.7.refs_0_), calls=%async_computation | async-start | bytes 4194304 | tf_op jit(solution)/shard_map/all_to_all | solution.py:227
  93.0 0.0 copy-done.14
  93.0 0.0 copy-start.12
  93.0 0.1 slice.13
  93.1 0.0 copy-done.13
  93.1 0.1 slice.15
  93.2 0.0 copy-done.16
  93.2 0.1 maximum_multiply_fusion.1
  93.2 3.5 %fusion.y_ref = f32[512,512]{1,0:T(8,128)S(1)} fusion(f32[512,512]{1,0:T(8,128)} %constant.12.clone, f32[512]{0:T(512)S(1)} %get-tuple-element.11), kind=kOutput, calls=%fused_computation | convolution fusion | flops 1610874880 | bytes 2099200 | tf_op jit(solution)/shard_map/dot_general | solution.py:201
  96.7 0.0 copy-done.12
  96.7 1.9 fusion.2.x_ref
  98.6 3.9 %window.3 = f32[32,2,64,128]{3,2,1,0:T(8,128)S(1)} custom-call(f32[512,512]{1,0:T(8,128)S(1)} %fusion.2.x_ref, f32[512,512]{1,0:T(8,128)S(1)} %fusion.y_ref, f32[32,2,64,128]{3,2,1,0:T(8,128)S(1)} %all-to-all-done.2.plane_ref), custom_call_target="tpu_custom_call" | custom-call | flops 3221225472 | bytes 4194304 | tf_op jit(solution)/shard_map/window/pallas_call | solution.py:134
  102.5 0.0 copy-start.3
  102.5 1.3 copy-done.3
  103.8 1.0 copy-done.4
  104.8 35.4 %all-to-all-done.plane_ref = f32[32,2,64,128]{3,2,1,0:T(8,128)} async-done(((f32[32,2,64,128]{3,2,1,0:T(8,128)}), f32[32,2,64,128]{3,2,1,0:T(8,128)}, u32[]{:S(2)}, u32[]{:S(2)}) %all-to-all-start) | async-done | bytes 2097184 | tf_op jit(solution)/shard_map/all_to_all | solution.py:227
  140.2 5.6 %all-to-all-start.3 = ((f32[32,2,64,128]{3,2,1,0:T(8,128)}), f32[32,2,64,128]{3,2,1,0:T(8,128)S(1)}, u32[]{:S(2)}, u32[]{:S(2)}) async-start(f32[32,2,64,128]{3,2,1,0:T(8,128)} %copy-done.3), calls=%async_computation.3 | async-start | bytes 4194304 | tf_op jit(solution)/shard_map/all_to_all | solution.py:229
  145.8 1.2 copy-done.5
  147.1 5.0 %window.2 = f32[32,2,64,128]{3,2,1,0:T(8,128)S(1)} custom-call(f32[512,512]{1,0:T(8,128)S(1)} %copy-done.5, f32[512,512]{1,0:T(8,128)S(1)} %fusion.y_ref, f32[32,2,64,128]{3,2,1,0:T(8,128)} %all-to-all-done.plane_ref), custom_call_target="tpu_custom_call" | custom-call | flops 3221225472 | bytes 4194304 | tf_op jit(solution)/shard_map/window/pallas_call | solution.py:134
  152.0 0.0 copy-start.2
  152.0 1.3 copy-done.2
  153.4 39.6 %all-to-all-done.3.refs_1_ = f32[32,2,64,128]{3,2,1,0:T(8,128)S(1)} async-done(((f32[32,2,64,128]{3,2,1,0:T(8,128)}), f32[32,2,64,128]{3,2,1,0:T(8,128)S(1)}, u32[]{:S(2)}, u32[]{:S(2)}) %all-to-all-start.3) | async-done | bytes 2097184 | tf_op jit(solution)/shard_map/all_to_all | solution.py:229
  193.0 6.3 %all-to-all-start.1 = ((f32[32,2,64,128]{3,2,1,0:T(8,128)}), f32[32,2,64,128]{3,2,1,0:T(8,128)}, u32[]{:S(2)}, u32[]{:S(2)}) async-start(f32[32,2,64,128]{3,2,1,0:T(8,128)} %copy-done.2), calls=%async_computation.1 | async-start | bytes 4194304 | tf_op jit(solution)/shard_map/all_to_all | solution.py:229
  199.3 0.1 copy.14
  199.4 0.1 reshape.18
  199.5 0.1 reduce_sum.28
  199.6 0.1 select_reduce_fusion
  199.7 56.3 %all-reduce = f32[8]{0:T(128)S(1)} all-reduce(f32[8]{0:T(128)S(1)} %broadcast_multiply_fusion.1), channel_id=2, replica_groups=mesh['gx'=4,'gy'=8] {'gy'}, use_global_device_ids=true, to_apply=%region_3.4.clone | all-reduce | flops 8 | bytes 64
  256.1 0.0 copy-done.17
  256.1 0.6 dynamic-slice
  256.7 1.2 dynamic-slice.1
  257.9 9.8 %restore.2 = f32[128,64,128]{2,1,0:T(8,128)} custom-call(f32[32,2,64,128]{3,2,1,0:T(8,128)} %get-tuple-element.7.refs_0_, f32[32,2,64,128]{3,2,1,0:T(8,128)} %get-tuple-element.8.refs_1_), custom_call_target="tpu_custom_call" | custom-call | flops 1073741824 | bytes 8388608 | tf_op jit(solution)/shard_map/restore/pallas_call | solution.py:174
  267.7 0.0 all-to-all-done.1.refs_0_
  267.7 9.4 %restore.3 = f32[128,64,128]{2,1,0:T(8,128)} custom-call(f32[32,2,64,128]{3,2,1,0:T(8,128)} %all-to-all-done.1.refs_0_, f32[32,2,64,128]{3,2,1,0:T(8,128)S(1)} %all-to-all-done.3.refs_1_), custom_call_target="tpu_custom_call" | custom-call | flops 1073741824 | bytes 8388608 | tf_op jit(solution)/shard_map/restore/pallas_call | solution.py:174
  (17 shorter events, 0.1 us)
Async XLA Ops:
  0.6 2.2 copy-start
  2.8 0.9 copy-start.6
  3.7 0.7 copy-start.8
  4.4 0.7 copy-start.10
  33.4 6.1 %copy-start.7 = (s32[128,64,4]{0,2,1:T(4,128)S(1)}, s32[128,64,4]{0,2,1:T(4,128)}, u32[]{:S(2)}) copy-start(s32[128,64,4]{0,2,1:T(4,128)} %param.10) | copy-start | bytes 393220
  33.4 6.1 %copy-start.9 = (bf16[128,64]{0,1:T(8,128)(2,1)S(1)}, bf16[128,64]{0,1:T(8,128)(2,1)}, u32[]{:S(2)}) copy-start(bf16[128,64]{0,1:T(8,128)(2,1)} %param.11) | copy-start | bytes 49156
  33.4 6.1 %copy-start.11 = (s32[4,2,4]{2,1,0:T(2,128)S(1)}, s32[4,2,4]{2,1,0:T(2,128)}, u32[]{:S(2)}) copy-start(s32[4,2,4]{2,1,0:T(2,128)} %mask_ref.3) | copy-start | bytes 388
  33.4 53.1 %all-to-all-start.2 = ((f32[32,2,64,128]{3,2,1,0:T(8,128)}), f32[32,2,64,128]{3,2,1,0:T(8,128)S(1)}, u32[]{:S(2)}, u32[]{:S(2)}) async-start(f32[32,2,64,128]{3,2,1,0:T(8,128)} %get-tuple-element.8.refs_1_), calls=%async_computation.2 | async-start | bytes 4194304 | tf_op jit(solution)/shard_map/all_to_all | solution.py:227
  39.5 2.2 copy-start.1
  86.5 6.5 %copy-start.14 = (f32[512]{0:T(512)S(1)}, f32[512]{0:T(512)}, u32[]{:S(2)}) copy-start(f32[512]{0:T(512)} %param.14) | copy-start | bytes 6148
  86.5 6.6 %copy-start.13 = (f32[512]{0:T(512)S(1)}, f32[512]{0:T(512)}, u32[]{:S(2)}) copy-start(f32[512]{0:T(512)} %param.15) | copy-start | bytes 6148
  86.5 6.6 %copy-start.16 = (f32[512]{0:T(512)S(1)}, f32[512]{0:T(512)}, u32[]{:S(2)}) copy-start(f32[512]{0:T(512)} %constant.13.clone) | copy-start | bytes 6148
  86.5 53.7 %all-to-all-start = ((f32[32,2,64,128]{3,2,1,0:T(8,128)}), f32[32,2,64,128]{3,2,1,0:T(8,128)}, u32[]{:S(2)}, u32[]{:S(2)}) async-start(f32[32,2,64,128]{3,2,1,0:T(8,128)} %get-tuple-element.7.refs_0_), calls=%async_computation | async-start | bytes 4194304 | tf_op jit(solution)/shard_map/all_to_all | solution.py:227
  93.0 3.7 %copy-start.12 = (f32[512,512]{1,0:T(8,128)S(1)}, f32[512,512]{1,0:T(8,128)}, u32[]{:S(2)}) copy-start(f32[512,512]{1,0:T(8,128)} %constant.12.clone) | copy-start | bytes 3145732
  102.5 1.3 copy-start.3
  103.8 1.0 copy-start.4
  140.2 52.8 %all-to-all-start.3 = ((f32[32,2,64,128]{3,2,1,0:T(8,128)}), f32[32,2,64,128]{3,2,1,0:T(8,128)S(1)}, u32[]{:S(2)}, u32[]{:S(2)}) async-start(f32[32,2,64,128]{3,2,1,0:T(8,128)} %copy-done.3), calls=%async_computation.3 | async-start | bytes 4194304 | tf_op jit(solution)/shard_map/all_to_all | solution.py:229
  145.8 1.2 copy-start.5
  152.0 1.4 copy-start.2
  153.4 45.9 %copy-start.15 = (s32[4,2,4]{2,1,0:T(2,128)S(1)}, s32[4,2,4]{2,1,0:T(2,128)}, u32[]{:S(2)}) copy-start(s32[4,2,4]{2,1,0:T(2,128)} %param.13) | copy-start | bytes 388
  153.4 102.7 %copy-start.17 = (u32[32]{0:T(128)S(1)}, u32[32]{0:T(128)}, u32[]{:S(2)}) copy-start(u32[32]{0:T(128)} %constant.18) | copy-start | bytes 388
  193.0 74.7 %all-to-all-start.1 = ((f32[32,2,64,128]{3,2,1,0:T(8,128)}), f32[32,2,64,128]{3,2,1,0:T(8,128)}, u32[]{:S(2)}, u32[]{:S(2)}) async-start(f32[32,2,64,128]{3,2,1,0:T(8,128)} %copy-done.2), calls=%async_computation.1 | async-start | bytes 4194304 | tf_op jit(solution)/shard_map/all_to_all | solution.py:229

commit v2 on v1

--- a/solution.py
+++ b/solution.py
@@ -9,15 +9,15 @@
 from jax.sharding import PartitionSpec as P
 
 STEEPNESS = 3.0
-ROWS = 8
-VMEM_BYTES = 40 * 1024 * 1024
+ROWS = 16
+UNROLL = 4
 
 
 def node_grid(nodes):
     return np.float32(-2.5) + np.float32(5.0) * np.arange(nodes, dtype=np.float32) / np.float32(nodes - 1)
 
 
-def evaluate_kernel(run_first, runs, edge, devices, mask_ref, field_ref, bins_ref, rate_ref, cells_ref, sums_ref, row_scratch, field_scratch):
+def evaluate_kernel(run_first, runs, edge, devices, mask_ref, field_ref, bins_ref, rate_ref, cells_ref, sums_ref, row_scratch):
     step = pl.program_id(0)
     size_x, rows, size_z = field_ref.shape
     nodes, levels = rate_ref.shape
@@ -44,24 +44,31 @@
             onehot = (level == bins_ref[y, pl.ds(run_first + run, 1), :]).astype(jnp.bfloat16)
             row_scratch[run, y] = jnp.dot(rate_ref[...], onehot, preferred_element_type=jnp.float32) * active
 
-    def one_row(y, carry):
-        turned = field[pl.ds(y, size_x, stride=rows), :].T
-        scaled = (turned * (0.5 * STEEPNESS))[run_first * edge : (run_first + runs) * edge]
-        for run in range(runs):
-            values = scaled[run * edge : (run + 1) * edge]
-            total = jnp.broadcast_to(jnp.sum(row_scratch[run, y], axis=0, keepdims=True), values.shape)
-            for q in range(nodes):
-                rate = row_scratch[run, y, pl.ds(q, 1), :]
-                total = total + rate * jnp.tanh(values - half_nodes[q])
-            plane, first = divmod(run * edge, devices)
-            cells[pl.ds(first * planes * rows + plane * rows + y, edge, stride=planes * rows), :] = total
-            part = total[0:8]
-            for k in range(8, edge, 8):
-                part = part + total[k : k + 8]
-            sums_ref[0, run] += part
+    first_z = run_first * edge
+    last_z = first_z + runs * edge
+
+    def some_rows(pair, carry):
+        for y in [pair * UNROLL + k for k in range(UNROLL)]:
+            if first_z == 0:
+                turned = field[pl.ds(y, size_x, stride=rows), :][:, :last_z].T
+            else:
+                turned = field[pl.ds(y, size_x, stride=rows), :].T[first_z:last_z]
+            scaled = turned * (0.5 * STEEPNESS)
+            for run in range(runs):
+                values = scaled[run * edge : (run + 1) * edge]
+                total = jnp.broadcast_to(jnp.sum(row_scratch[run, y], axis=0, keepdims=True), values.shape)
+                for q in range(nodes):
+                    rate = row_scratch[run, y, pl.ds(q, 1), :]
+                    total = total + rate * jnp.tanh(values - half_nodes[q])
+                plane, first = divmod(run * edge, devices)
+                cells[pl.ds(first * planes * rows + plane * rows + y, edge, stride=planes * rows), :] = total
+                part = total[0:8]
+                for k in range(8, edge, 8):
+                    part = part + total[k : k + 8]
+                sums_ref[0, run] += part
         return carry
 
-    lax.fori_loop(0, rows, one_row, 0)
+    lax.fori_loop(0, rows // UNROLL, some_rows, 0)
 
 
 def evaluate(log_crit, bins, rates, tile_mask, run_first, runs, devices):
@@ -90,12 +97,10 @@
         ],
         scratch_shapes=[
             pltpu.VMEM((runs, ROWS, nodes, size_x), jnp.float32),
-            pltpu.VMEM((size_z, size_x), jnp.float32),
         ],
         cost_estimate=pl.CostEstimate(
             flops=runs * edge * size_x * size_y * nodes * 4, bytes_accessed=6 << 20, transcendentals=0
         ),
-        compiler_params=pltpu.CompilerParams(vmem_limit_bytes=VMEM_BYTES),
         name="evaluate",
     )(tile_mask, log_crit, bins, rates)
 
@@ -144,7 +149,6 @@
         cost_estimate=pl.CostEstimate(
             flops=count * 6 * size_x * size_y * (size_x + size_y), bytes_accessed=4 << 20, transcendentals=0
         ),
-        compiler_params=pltpu.CompilerParams(vmem_limit_bytes=VMEM_BYTES),
         name="window",
     )(matrix_x, matrix_y, planes)
 
@@ -154,7 +158,7 @@
     size_x, rows, size_z = out_ref.shape
     out = out_ref.reshape(size_x * rows, size_z)
 
-    def one_row(y, carry):
+    for y in range(rows):
         pieces = []
         for part in parts:
             devices, planes = part.shape[:2]
@@ -163,9 +167,6 @@
                 pieces.append(flat[pl.ds(plane * rows + y, devices, stride=planes * rows), :])
         whole = pieces[0] if len(pieces) == 1 else jnp.concatenate(pieces, axis=0)
         out[pl.ds(y, size_x, stride=rows), :] = whole.T
-        return carry
-
-    lax.fori_loop(0, rows, one_row, 0)
 
 
 def restore(parts, edge):
@@ -180,7 +181,6 @@
         out_specs=pl.BlockSpec((size_x, ROWS, size_z), lambda j: (0, j, 0)),
         out_shape=jax.ShapeDtypeStruct((size_x, size_y, size_z), jnp.float32),
         cost_estimate=pl.CostEstimate(flops=1 << 30, bytes_accessed=8 << 20, transcendentals=0),
-        compiler_params=pltpu.CompilerParams(vmem_limit_bytes=VMEM_BYTES),
         name="restore",
     )(*parts)
 
@@ -224,19 +224,22 @@
     exchange = functools.partial(
         lax.all_to_all, axis_name=("gx", "gy"), split_axis=0, concat_axis=0, tiled=True
     )
-    pencils = [exchange(part) for part in cells]
-    filtered = [apply_window(part, matrix_x, matrix_y, span_x, span_y) for part in pencils]
-    returned = [exchange(part) for part in filtered]
-    recomb = restore(cells, edge)
-    smoothed = restore(returned, edge)
     tile_sums = jnp.concatenate(sums, axis=1).sum(axis=2)
     tile_means = tile_sums.reshape(blocks_y, blocks_z, blocks_x, edge).sum(axis=3) / (edge * edge * edge)
     route = tile_route.transpose(1, 2, 0)
     workers = jnp.arange(span_y, dtype=jnp.int32)
     shares = jnp.where(route[..., None] == workers, tile_means[..., None], 0.0)
     contribution = shares.sum(axis=(0, 1, 2)) / (tile_count // 2)
-    load = lax.psum_scatter(contribution, "gy", scatter_dimension=0, tiled=True)
-    return recomb, smoothed, load.reshape(1, 1)
+    pencils = [exchange(part) for part in cells]
+    recomb = restore(cells, edge)
+    filtered = [apply_window(part, matrix_x, matrix_y, span_x, span_y) for part in pencils]
+    filtered[0], recomb = lax.optimization_barrier((filtered[0], recomb))
+    filtered[-1], contribution = lax.optimization_barrier((filtered[-1], contribution))
+    returned = [exchange(part) for part in filtered]
+    mine = workers == lax.axis_index("gy")
+    load = jnp.sum(jnp.where(mine, lax.psum(contribution, "gy"), 0.0)).reshape(1, 1)
+    smoothed = restore(returned, edge)
+    return recomb, smoothed, load
 
 
 def split_runs(size_z, edge, devices):
@@ -244,8 +247,7 @@
     smallest = max(1, devices // edge)
     if smallest * 2 > runs:
         return ((0, runs),)
-    half = runs // 2
-    return ((0, half), (half, runs - half))
+    return ((0, smallest), (smallest, runs - smallest))
 
 
 def solution(mesh):

time: 278 us -> 257 us (0.924)
  blocking collectives: 56.3 us -> 79.3 us
  waiting for transfers between devices: 92.7 us -> 70 us
  local copies, waits for them, and re-layouts: 13.7 us -> 3.97 us
  Pallas kernels: 83.4 us -> 73.7 us
    psum x0 -> x1, blocking collectives: none -> 79.3 us  [on_device(): lax.psum(contribution, 'gy')]
    unnamed x1 -> x0, blocking collectives: 56.3 us -> none
    all_to_all x2, waiting for transfers between devices: 39.6 us -> 17.3 us  [on_device(): returned = [exchange(part) for part in filtered]]
    unnamed x38 -> x20, local copies, waits for them, and re-layouts: 13.4 us -> 3.64 us
    pallas_call x2, Pallas kernels: 19.1 us -> 11.7 us  [restore(): pl.pallas_call(functools.partial(restore_kernel, edge, len(parts)), grid=...]
    pallas_call x2, Pallas kernels: 55.4 us -> 49.1 us  [evaluate(): pl.pallas_call(functools.partial(evaluate_kernel, run_first, runs, edge,...]
    pallas_call x2, Pallas kernels: 8.87 us -> 13 us  [apply_window(): pl.pallas_call(functools.partial(window_kernel, span_x, span_y), grid=(co...]
  transfers between devices with their start and end apart: 4 -> 4, of which waited for: 3 -> 2; matrix products, arithmetic and copies ran while one was open for 3% -> 3% of each run, Pallas kernels for 17% -> 21%
where the time goes in v2:
time: 257 us
  blocking collectives  79.3 us (31%)
  Pallas kernels  73.7 us (29%)
  waiting for transfers between devices  70 us (27%)
  starting transfers between devices  22.5 us (9%)
  matrix products  5.7 us (2%)
  local copies, waits for them, and re-layouts  3.97 us (2%)
    psum x1, blocking collectives, on_device(): lax.psum(contribution, 'gy')  79.3 us
    all_to_all x2, waiting for transfers between devices, on_device(): pencils = [exchange(part) for part in cells]  52.7 us
    pallas_call x2, Pallas kernels, evaluate(): pl.pallas_call(functools.partial(evaluate_kernel, run_first, runs, edge,...  49.1 us
    all_to_all x2, waiting for transfers between devices, on_device(): returned = [exchange(part) for part in filtered]  17.3 us
    pallas_call x2, Pallas kernels, apply_window(): pl.pallas_call(functools.partial(window_kernel, span_x, span_y), grid=(co...  13 us
    all_to_all x2, starting transfers between devices, on_device(): pencils = [exchange(part) for part in cells]  11.9 us
    pallas_call x2, Pallas kernels, restore(): pl.pallas_call(functools.partial(restore_kernel, edge, len(parts)), grid=...  11.7 us
    all_to_all x2, starting transfers between devices, on_device(): returned = [exchange(part) for part in filtered]  10.5 us
  transfers between devices with their start and end apart: 4, of which 2 were waited for; matrix products, arithmetic and copies ran while one was open for 3% of the time, Pallas kernels for 21%

profile of v2, /device:TPU:8, one launch (start us, length us, event | category | flops | bytes accessed | tf_op | source)
XLA Modules:
  0.0 256.8 jit_solution(3666447066440989254)
XLA Ops:
  0.6 13.9 %evaluate.2 = (f32[32,1,64,128]{3,2,1,0:T(8,128)}, f32[2,1,8,128]{3,2,1,0:T(8,128)}) custom-call(s32[4,2,4]{2,1,0:T(2,128)} %mask_ref.3, f32[128,64,128]{2,1,0:T(8,128)} %field_ref.3, s32[64,4,128]{2,1,0:T(4,128)} %bitcast.8, bf16[64,128]{1,0:T(8,128)(2,1)} %bitcast.10), custom_call_target="tpu_custom_call" | custom-call | flops 67108864 | bytes 6291456 | tf_op jit(solution)/shard_map/evaluate/pallas_call | solution.py:81
  14.5 6.0 %all-to-all-start = ((f32[32,1,64,128]{3,2,1,0:T(8,128)}), f32[32,1,64,128]{3,2,1,0:T(8,128)S(1)}, u32[]{:S(2)}, u32[]{:S(2)}) async-start(f32[32,1,64,128]{3,2,1,0:T(8,128)} %get-tuple-element.11.refs_0_), calls=%async_computation | async-start | bytes 2097152 | tf_op jit(solution)/shard_map/all_to_all | solution.py:233
  20.6 35.1 %evaluate.3 = (f32[32,3,64,128]{3,2,1,0:T(8,128)}, f32[2,3,8,128]{3,2,1,0:T(8,128)}) custom-call(s32[4,2,4]{2,1,0:T(2,128)} %mask_ref.3, f32[128,64,128]{2,1,0:T(8,128)} %field_ref.3, s32[64,4,128]{2,1,0:T(4,128)} %bitcast.9, bf16[64,128]{1,0:T(8,128)(2,1)} %bitcast.11), custom_call_target="tpu_custom_call" | custom-call | flops 201326592 | bytes 6291456 | tf_op jit(solution)/shard_map/evaluate/pallas_call | solution.py:81
  55.7 0.0 all-to-all-done.plane_ref
  55.7 0.0 copy-start.3
  55.7 0.0 copy-start.7
  55.8 0.0 copy-start.6
  55.8 1.0 copy-done.3
  56.7 5.9 %all-to-all-start.2 = ((f32[32,3,64,128]{3,2,1,0:T(8,128)}), f32[32,3,64,128]{3,2,1,0:T(8,128)}, u32[]{:S(2)}, u32[]{:S(2)}) async-start(f32[32,3,64,128]{3,2,1,0:T(8,128)} %get-tuple-element.12.refs_1_), calls=%async_computation.2 | async-start | bytes 6291456 | tf_op jit(solution)/shard_map/all_to_all | solution.py:233
  62.6 0.0 copy-done.7
  62.6 0.1 slice.13
  62.7 0.0 copy-done.6
  62.7 0.1 slice.15
  62.8 0.0 copy-start.9
  62.8 0.0 copy-start
  62.8 5.9 %restore.2 = f32[128,64,128]{2,1,0:T(8,128)} custom-call(f32[32,1,64,128]{3,2,1,0:T(8,128)} %get-tuple-element.11.refs_0_, f32[32,3,64,128]{3,2,1,0:T(8,128)} %get-tuple-element.12.refs_1_), custom_call_target="tpu_custom_call" | custom-call | flops 1073741824 | bytes 8388608 | tf_op jit(solution)/shard_map/restore/pallas_call | solution.py:175
  68.7 0.0 copy-done.9
  68.7 0.1 maximum_multiply_fusion.1
  68.7 0.0 copy-done
  68.7 2.8 %fusion.y_ref = f32[512,512]{1,0:T(8,128)} fusion(f32[512,512]{1,0:T(8,128)S(1)} %copy-done, f32[512]{0:T(512)S(1)} %get-tuple-element.19), kind=kOutput, calls=%fused_computation | convolution fusion | flops 1610874880 | bytes 2099200 | tf_op jit(solution)/shard_map/dot_general | solution.py:201
  71.6 2.9 %fusion.2.x_ref = f32[512,512]{1,0:T(8,128)} fusion(f32[512,512]{1,0:T(8,128)S(1)} %copy-done, f32[512]{0:T(512)S(1)} %get-tuple-element.20), kind=kOutput, calls=%fused_computation.2 | convolution fusion | flops 1610874880 | bytes 2099200 | tf_op jit(solution)/shard_map/dot_general | solution.py:201
  74.4 0.0 copy-start.8
  74.4 0.0 copy-start.4
  74.4 0.0 copy-start.5
  74.5 4.7 %window.2 = f32[32,1,64,128]{3,2,1,0:T(8,128)} custom-call(f32[512,512]{1,0:T(8,128)} %fusion.2.x_ref, f32[512,512]{1,0:T(8,128)} %fusion.y_ref, f32[32,1,64,128]{3,2,1,0:T(8,128)} %copy-done.3), custom_call_target="tpu_custom_call" | custom-call | flops 1610612736 | bytes 4194304 | tf_op jit(solution)/shard_map/window/pallas_call | solution.py:139
  79.1 52.7 %all-to-all-done.2.plane_ref = f32[32,3,64,128]{3,2,1,0:T(8,128)} async-done(((f32[32,3,64,128]{3,2,1,0:T(8,128)}), f32[32,3,64,128]{3,2,1,0:T(8,128)}, u32[]{:S(2)}, u32[]{:S(2)}) %all-to-all-start.2) | async-done | bytes 3145760 | tf_op jit(solution)/shard_map/all_to_all | solution.py:233
  131.8 6.4 %all-to-all-start.1 = ((f32[32,1,64,128]{3,2,1,0:T(8,128)}), f32[32,1,64,128]{3,2,1,0:T(8,128)S(1)}, u32[]{:S(2)}, u32[]{:S(2)}) async-start(f32[32,1,64,128]{3,2,1,0:T(8,128)} %window.2), calls=%async_computation.1 | async-start | bytes 2097152 | tf_op jit(solution)/shard_map/all_to_all | solution.py:238
  138.2 0.0 copy-done.8
  138.2 0.1 copy.13
  138.3 0.0 copy-done.4
  138.3 0.0 copy-done.5
  138.3 0.1 reshape.18
  138.4 0.1 reduce_sum.37
  138.5 0.1 select_reduce_fusion
  138.6 8.3 %window.3 = f32[32,3,64,128]{3,2,1,0:T(8,128)} custom-call(f32[512,512]{1,0:T(8,128)} %fusion.2.x_ref, f32[512,512]{1,0:T(8,128)} %fusion.y_ref, f32[32,3,64,128]{3,2,1,0:T(8,128)} %all-to-all-done.2.plane_ref), custom_call_target="tpu_custom_call" | custom-call | flops 4831838208 | bytes 4194304 | tf_op jit(solution)/shard_map/window/pallas_call | solution.py:139
  146.9 17.3 %all-to-all-done.1.refs_0_ = f32[32,1,64,128]{3,2,1,0:T(8,128)S(1)} async-done(((f32[32,1,64,128]{3,2,1,0:T(8,128)}), f32[32,1,64,128]{3,2,1,0:T(8,128)S(1)}, u32[]{:S(2)}, u32[]{:S(2)}) %all-to-all-start.1) | async-done | bytes 1048608 | tf_op jit(solution)/shard_map/all_to_all | solution.py:238
  164.3 0.0 copy-start.2
  164.3 1.0 copy-done.2
  165.3 4.2 %all-to-all-start.3 = ((f32[32,3,64,128]{3,2,1,0:T(8,128)}), f32[32,3,64,128]{3,2,1,0:T(8,128)S(1)}, u32[]{:S(2)}, u32[]{:S(2)}) async-start(f32[32,3,64,128]{3,2,1,0:T(8,128)} %window.3), calls=%async_computation.3 | async-start | bytes 6291456 | tf_op jit(solution)/shard_map/all_to_all | solution.py:238
  169.4 79.3 %psum.7 = f32[8]{0:T(128)S(1)} all-reduce(f32[8]{0:T(128)S(1)} %broadcast_multiply_fusion.1), channel_id=1, replica_groups=mesh['gx'=4,'gy'=8] {'gy'}, use_global_device_ids=true, to_apply=%region_3.4 | all-reduce | flops 8 | bytes 64 | tf_op jit(solution)/shard_map/psum | solution.py:240
  248.7 0.6 fusion.6
  249.3 0.0 all-to-all-done.3.refs_1_
  249.3 0.0 copy-start.1
  249.3 1.6 copy-done.1
  251.0 5.8 %restore.3 = f32[128,64,128]{2,1,0:T(8,128)} custom-call(f32[32,1,64,128]{3,2,1,0:T(8,128)} %copy-done.2, f32[32,3,64,128]{3,2,1,0:T(8,128)} %copy-done.1), custom_call_target="tpu_custom_call" | custom-call | flops 1073741824 | bytes 8388608 | tf_op jit(solution)/shard_map/restore/pallas_call | solution.py:175
  (3 shorter events, 0.0 us)
Async XLA Ops:
  14.5 41.2 %all-to-all-start = ((f32[32,1,64,128]{3,2,1,0:T(8,128)}), f32[32,1,64,128]{3,2,1,0:T(8,128)S(1)}, u32[]{:S(2)}, u32[]{:S(2)}) async-start(f32[32,1,64,128]{3,2,1,0:T(8,128)} %get-tuple-element.11.refs_0_), calls=%async_computation | async-start | bytes 2097152 | tf_op jit(solution)/shard_map/all_to_all | solution.py:233
  55.7 1.0 copy-start.3
  55.7 6.9 %copy-start.7 = (f32[512]{0:T(512)S(1)}, f32[512]{0:T(512)}, u32[]{:S(2)}) copy-start(f32[512]{0:T(512)} %param.14) | copy-start | bytes 6148
  55.8 7.0 %copy-start.6 = (f32[512]{0:T(512)S(1)}, f32[512]{0:T(512)}, u32[]{:S(2)}) copy-start(f32[512]{0:T(512)} %param.15) | copy-start | bytes 6148
  56.7 75.1 %all-to-all-start.2 = ((f32[32,3,64,128]{3,2,1,0:T(8,128)}), f32[32,3,64,128]{3,2,1,0:T(8,128)}, u32[]{:S(2)}, u32[]{:S(2)}) async-start(f32[32,3,64,128]{3,2,1,0:T(8,128)} %get-tuple-element.12.refs_1_), calls=%async_computation.2 | async-start | bytes 6291456 | tf_op jit(solution)/shard_map/all_to_all | solution.py:233
  62.8 5.9 %copy-start.9 = (f32[512]{0:T(512)S(1)}, f32[512]{0:T(512)}, u32[]{:S(2)}) copy-start(f32[512]{0:T(512)} %constant.17.clone) | copy-start | bytes 6148
  62.8 6.0 %copy-start = (f32[512,512]{1,0:T(8,128)S(1)}, f32[512,512]{1,0:T(8,128)}, u32[]{:S(2)}) copy-start(f32[512,512]{1,0:T(8,128)} %constant.16.clone) | copy-start | bytes 3145732
  74.4 63.7 %copy-start.8 = (s32[4,2,4]{2,1,0:T(2,128)S(1)}, s32[4,2,4]{2,1,0:T(2,128)}, u32[]{:S(2)}) copy-start(s32[4,2,4]{2,1,0:T(2,128)} %param.13) | copy-start | bytes 388
  74.4 63.8 %copy-start.4 = (f32[2,3,8,128]{3,2,1,0:T(8,128)S(1)}, f32[2,3,8,128]{3,2,1,0:T(8,128)}, u32[]{:S(2)}) copy-start(f32[2,3,8,128]{3,2,1,0:T(8,128)} %get-tuple-element.16) | copy-start | bytes 73732
  74.4 63.9 %copy-start.5 = (f32[2,1,8,128]{3,2,1,0:T(8,128)S(1)}, f32[2,1,8,128]{3,2,1,0:T(8,128)}, u32[]{:S(2)}) copy-start(f32[2,1,8,128]{3,2,1,0:T(8,128)} %get-tuple-element.15) | copy-start | bytes 24580
  131.8 32.4 %all-to-all-start.1 = ((f32[32,1,64,128]{3,2,1,0:T(8,128)}), f32[32,1,64,128]{3,2,1,0:T(8,128)S(1)}, u32[]{:S(2)}, u32[]{:S(2)}) async-start(f32[32,1,64,128]{3,2,1,0:T(8,128)} %window.2), calls=%async_computation.1 | async-start | bytes 2097152 | tf_op jit(solution)/shard_map/all_to_all | solution.py:238
  164.3 1.0 copy-start.2
  165.3 84.1 %all-to-all-start.3 = ((f32[32,3,64,128]{3,2,1,0:T(8,128)}), f32[32,3,64,128]{3,2,1,0:T(8,128)S(1)}, u32[]{:S(2)}, u32[]{:S(2)}) async-start(f32[32,3,64,128]{3,2,1,0:T(8,128)} %window.3), calls=%async_computation.3 | async-start | bytes 6291456 | tf_op jit(solution)/shard_map/all_to_all | solution.py:238
  249.3 1.7 copy-start.1

commit v3 on v2

--- a/solution.py
+++ b/solution.py
@@ -116,15 +116,23 @@
     return dot(left[0], right[0]) + (dot(left[0], right[1]) + dot(left[1], right[0]))
 
 
-def window_kernel(span_x, span_y, x_ref, y_ref, plane_ref, out_ref):
-    rows, lanes = plane_ref.shape[-2:]
-    plane = jnp.concatenate(
-        [
-            jnp.concatenate([plane_ref[i * span_y + j, 0] for i in range(span_x)], axis=1)
-            for j in range(span_y)
-        ],
-        axis=0,
-    )
+def window_kernel(span_x, span_y, first_planes, x_ref, y_ref, *refs):
+    plane_refs, out_ref = refs[:-1], refs[-1]
+    rows, lanes = out_ref.shape[-2:]
+    step = pl.program_id(0)
+
+    def assemble(ref):
+        return jnp.concatenate(
+            [
+                jnp.concatenate([ref[i * span_y + j, 0] for i in range(span_x)], axis=1)
+                for j in range(span_y)
+            ],
+            axis=0,
+        )
+
+    plane = assemble(plane_refs[0])
+    if len(plane_refs) == 2:
+        plane = jnp.where(step < first_planes, plane, assemble(plane_refs[1]))
     along_y = product(split(y_ref[...]), split(plane))
     both = product(split(along_y), split(x_ref[...]))
     for i in range(span_x):
@@ -132,25 +140,29 @@
             out_ref[i * span_y + j, 0] = both[j * rows : (j + 1) * rows, i * lanes : (i + 1) * lanes]
 
 
-def apply_window(planes, matrix_x, matrix_y, span_x, span_y):
-    devices, count, rows, lanes = planes.shape
+def apply_window(parts, matrix_x, matrix_y, span_x, span_y):
+    devices, first_planes, rows, lanes = parts[0].shape
+    count = sum(part.shape[1] for part in parts)
     size_x, size_y = matrix_x.shape[0], matrix_y.shape[0]
-    spec = pl.BlockSpec((devices, 1, rows, lanes), lambda p: (0, p, 0, 0))
+    block = (devices, 1, rows, lanes)
+    specs = [pl.BlockSpec(block, lambda p: (0, jnp.minimum(p, first_planes - 1), 0, 0))]
+    if len(parts) == 2:
+        specs.append(pl.BlockSpec(block, lambda p: (0, jnp.maximum(p - first_planes, 0), 0, 0)))
     return pl.pallas_call(
-        functools.partial(window_kernel, span_x, span_y),
+        functools.partial(window_kernel, span_x, span_y, first_planes),
         grid=(count,),
         in_specs=[
             pl.BlockSpec((size_x, size_x), lambda p: (0, 0)),
             pl.BlockSpec((size_y, size_y), lambda p: (0, 0)),
-            spec,
-        ],
-        out_specs=spec,
-        out_shape=jax.ShapeDtypeStruct(planes.shape, jnp.float32),
+            *specs,
+        ],
+        out_specs=pl.BlockSpec(block, lambda p: (0, p, 0, 0)),
+        out_shape=jax.ShapeDtypeStruct((devices, count, rows, lanes), jnp.float32),
         cost_estimate=pl.CostEstimate(
             flops=count * 6 * size_x * size_y * (size_x + size_y), bytes_accessed=4 << 20, transcendentals=0
         ),
         name="window",
-    )(matrix_x, matrix_y, planes)
+    )(matrix_x, matrix_y, *parts)
 
 
 def restore_kernel(edge, count, *refs):
@@ -181,6 +193,7 @@
         out_specs=pl.BlockSpec((size_x, ROWS, size_z), lambda j: (0, j, 0)),
         out_shape=jax.ShapeDtypeStruct((size_x, size_y, size_z), jnp.float32),
         cost_estimate=pl.CostEstimate(flops=1 << 30, bytes_accessed=8 << 20, transcendentals=0),
+        compiler_params=pltpu.CompilerParams(vmem_limit_bytes=16 << 20),
         name="restore",
     )(*parts)
 
@@ -232,8 +245,9 @@
     contribution = shares.sum(axis=(0, 1, 2)) / (tile_count // 2)
     pencils = [exchange(part) for part in cells]
     recomb = restore(cells, edge)
-    filtered = [apply_window(part, matrix_x, matrix_y, span_x, span_y) for part in pencils]
-    filtered[0], recomb = lax.optimization_barrier((filtered[0], recomb))
+    shares_of = [pencils] if len(pencils) < 3 else [pencils[:2], pencils[2:]]
+    filtered = [apply_window(parts, matrix_x, matrix_y, span_x, span_y) for parts in shares_of]
+    filtered[-1], recomb = lax.optimization_barrier((filtered[-1], recomb))
     filtered[-1], contribution = lax.optimization_barrier((filtered[-1], contribution))
     returned = [exchange(part) for part in filtered]
     mine = workers == lax.axis_index("gy")
@@ -245,9 +259,9 @@
 def split_runs(size_z, edge, devices):
     runs = size_z // edge
     smallest = max(1, devices // edge)
-    if smallest * 2 > runs:
+    if smallest * 4 != runs:
         return ((0, runs),)
-    return ((0, smallest), (smallest, runs - smallest))
+    return ((0, smallest), (smallest, 2 * smallest), (3 * smallest, smallest))
 
 
 def solution(mesh):

time: 257 us -> 253 us (0.984)
  waiting for transfers between devices: 70 us -> 60.6 us
  starting transfers between devices: 22.5 us -> 25.8 us
    all_to_all x2 -> x3, waiting for transfers between devices: 52.7 us -> 43.4 us  [on_device(): pencils = [exchange(part) for part in cells]]
    pallas_call x2 -> x3, Pallas kernels: 49.1 us -> 53.5 us  [evaluate(): pl.pallas_call(functools.partial(evaluate_kernel, run_first, runs, edge,...]
    all_to_all x2 -> x3, starting transfers between devices: 11.9 us -> 16 us  [on_device(): pencils = [exchange(part) for part in cells]]
    pallas_call x2, Pallas kernels: 11.7 us -> 8.17 us  [restore(): pl.pallas_call(functools.partial(restore_kernel, edge, len(parts)), grid=...]
  transfers between devices with their start and end apart: 4 -> 5, of which waited for: 2 -> 4; matrix products, arithmetic and copies ran while one was open for 3% -> 3% of each run, Pallas kernels for 21% -> 23%
where the time goes in v3:
time: 253 us; the launch traced here: 252 us
  blocking collectives  79.3 us (31%)
  Pallas kernels  75.1 us (30%)
  waiting for transfers between devices  60.6 us (24%)
  starting transfers between devices  25.8 us (10%)
  matrix products  5.7 us (2%)
  local copies, waits for them, and re-layouts  3.79 us (1%)
    psum x1, blocking collectives, on_device(): lax.psum(contribution, 'gy')  79.3 us
    pallas_call x3, Pallas kernels, evaluate(): pl.pallas_call(functools.partial(evaluate_kernel, run_first, runs, edge,...  53.5 us
    all_to_all x3, waiting for transfers between devices, on_device(): pencils = [exchange(part) for part in cells]  43.4 us
    all_to_all x2, waiting for transfers between devices, on_device(): returned = [exchange(part) for part in filtered]  17.3 us
    all_to_all x3, starting transfers between devices, on_device(): pencils = [exchange(part) for part in cells]  16 us
    pallas_call x2, Pallas kernels, apply_window(): pl.pallas_call(functools.partial(window_kernel, span_x, span_y, first_pla...  13.5 us
    all_to_all x2, starting transfers between devices, on_device(): returned = [exchange(part) for part in filtered]  9.73 us
    pallas_call x2, Pallas kernels, restore(): pl.pallas_call(functools.partial(restore_kernel, edge, len(parts)), grid=...  8.17 us
  transfers between devices with their start and end apart: 5, of which 4 were waited for; matrix products, arithmetic and copies ran while one was open for 3% of the time, Pallas kernels for 23%

profile of v3, /device:TPU:8, one launch (start us, length us, event | category | flops | bytes accessed | tf_op | source)
XLA Modules:
  0.0 252.0 jit_solution(96572463059679297)
XLA Ops:
  0.6 14.3 %evaluate.3 = (f32[32,1,64,128]{3,2,1,0:T(8,128)}, f32[2,1,8,128]{3,2,1,0:T(8,128)}) custom-call(s32[4,2,4]{2,1,0:T(2,128)} %mask_ref.5, f32[128,64,128]{2,1,0:T(8,128)} %field_ref.5, s32[64,4,128]{2,1,0:T(4,128)} %bitcast.8, bf16[64,128]{1,0:T(8,128)(2,1)} %bitcast.11), custom_call_target="tpu_custom_call" | custom-call | flops 67108864 | bytes 6291456 | tf_op jit(solution)/shard_map/evaluate/pallas_call | solution.py:81
  14.9 6.1 %all-to-all-start = ((f32[32,1,64,128]{3,2,1,0:T(8,128)}), f32[32,1,64,128]{3,2,1,0:T(8,128)S(1)}, u32[]{:S(2)}, u32[]{:S(2)}) async-start(f32[32,1,64,128]{3,2,1,0:T(8,128)} %get-tuple-element.13.refs_2_), calls=%async_computation | async-start | bytes 2097152 | tf_op jit(solution)/shard_map/all_to_all | solution.py:246
  21.0 13.9 %evaluate.4 = (f32[32,1,64,128]{3,2,1,0:T(8,128)}, f32[2,1,8,128]{3,2,1,0:T(8,128)}) custom-call(s32[4,2,4]{2,1,0:T(2,128)} %mask_ref.5, f32[128,64,128]{2,1,0:T(8,128)} %field_ref.5, s32[64,4,128]{2,1,0:T(4,128)} %bitcast.9, bf16[64,128]{1,0:T(8,128)(2,1)} %bitcast.12), custom_call_target="tpu_custom_call" | custom-call | flops 67108864 | bytes 6291456 | tf_op jit(solution)/shard_map/evaluate/pallas_call | solution.py:81
  34.8 12.1 %all-to-all-done.refs_0_ = f32[32,1,64,128]{3,2,1,0:T(8,128)S(1)} async-done(((f32[32,1,64,128]{3,2,1,0:T(8,128)}), f32[32,1,64,128]{3,2,1,0:T(8,128)S(1)}, u32[]{:S(2)}, u32[]{:S(2)}) %all-to-all-start) | async-done | bytes 1048608 | tf_op jit(solution)/shard_map/all_to_all | solution.py:246
  47.0 4.7 %all-to-all-start.1 = ((f32[32,1,64,128]{3,2,1,0:T(8,128)}), f32[32,1,64,128]{3,2,1,0:T(8,128)}, u32[]{:S(2)}, u32[]{:S(2)}) async-start(f32[32,1,64,128]{3,2,1,0:T(8,128)} %get-tuple-element.14.refs_0_), calls=%async_computation.1 | async-start | bytes 2097152 | tf_op jit(solution)/shard_map/all_to_all | solution.py:246
  51.7 0.0 copy-done.6
  51.7 25.3 %evaluate.5 = (f32[32,2,64,128]{3,2,1,0:T(8,128)}, f32[2,2,8,128]{3,2,1,0:T(8,128)}) custom-call(s32[4,2,4]{2,1,0:T(2,128)} %mask_ref.5, f32[128,64,128]{2,1,0:T(8,128)} %field_ref.5, s32[64,4,128]{2,1,0:T(4,128)} %bitcast.10, bf16[64,128]{1,0:T(8,128)(2,1)} %bitcast.13), custom_call_target="tpu_custom_call" | custom-call | flops 134217728 | bytes 6291456 | tf_op jit(solution)/shard_map/evaluate/pallas_call | solution.py:81
  77.0 0.0 copy-start.7
  77.1 0.0 copy-start.8
  77.1 0.0 copy-start.9
  77.1 0.0 copy-start.12
  77.1 0.0 copy-start
  77.1 0.0 copy-start.1
  77.1 0.7 all-to-all-done.1.refs_0_
  77.8 5.3 %all-to-all-start.2 = ((f32[32,2,64,128]{3,2,1,0:T(8,128)}), f32[32,2,64,128]{3,2,1,0:T(8,128)}, u32[]{:S(2)}, u32[]{:S(2)}) async-start(f32[32,2,64,128]{3,2,1,0:T(8,128)} %get-tuple-element.15.refs_1_), calls=%async_computation.2 | async-start | bytes 4194304 | tf_op jit(solution)/shard_map/all_to_all | solution.py:246
  83.1 0.0 copy-done.11
  83.1 0.1 slice.13
  83.2 0.0 copy-done.10
  83.2 0.1 slice.15
  83.3 0.0 copy-done.7
  83.3 0.0 copy-done.8
  83.3 0.0 copy-done.9
  83.3 0.1 reshape.18
  83.4 0.0 copy-done.12
  83.4 0.1 copy.13
  83.5 0.1 reduce_sum.37
  83.6 0.0 copy-done
  83.6 0.0 copy-done.1
  83.6 0.0 copy-start.2
  83.6 1.2 copy-done.2
  84.8 4.3 %restore.2 = f32[128,64,128]{2,1,0:T(8,128)} custom-call(f32[32,1,64,128]{3,2,1,0:T(8,128)S(1)} %copy-done.2, f32[32,2,64,128]{3,2,1,0:T(8,128)S(1)} %copy-done, f32[32,1,64,128]{3,2,1,0:T(8,128)S(1)} %copy-done.1), custom_call_target="tpu_custom_call" | custom-call | flops 1073741824 | bytes 8388608 | tf_op jit(solution)/shard_map/restore/pallas_call | solution.py:187
  89.1 0.1 select_reduce_fusion
  89.2 0.0 copy-done.13
  89.2 0.1 maximum_multiply_fusion.1
  89.3 2.9 %fusion.y_ref = f32[512,512]{1,0:T(8,128)} fusion(f32[512,512]{1,0:T(8,128)S(1)} %copy-done.5, f32[512]{0:T(512)S(1)} %get-tuple-element.23), kind=kOutput, calls=%fused_computation | convolution fusion | flops 1610874880 | bytes 2099200 | tf_op jit(solution)/shard_map/dot_general | solution.py:214
  92.2 2.8 %fusion.2.x_ref = f32[512,512]{1,0:T(8,128)} fusion(f32[512,512]{1,0:T(8,128)S(1)} %copy-done.5, f32[512]{0:T(512)S(1)} %get-tuple-element.24), kind=kOutput, calls=%fused_computation.2 | convolution fusion | flops 1610874880 | bytes 2099200 | tf_op jit(solution)/shard_map/dot_general | solution.py:214
  95.0 4.7 %window.2 = f32[32,1,64,128]{3,2,1,0:T(8,128)} custom-call(f32[512,512]{1,0:T(8,128)} %fusion.2.x_ref, f32[512,512]{1,0:T(8,128)} %fusion.y_ref, f32[32,1,64,128]{3,2,1,0:T(8,128)} %copy-done.6), custom_call_target="tpu_custom_call" | custom-call | flops 1610612736 | bytes 4194304 | tf_op jit(solution)/shard_map/window/pallas_call | solution.py:151
  99.7 30.5 %all-to-all-done.2.refs_1_ = f32[32,2,64,128]{3,2,1,0:T(8,128)} async-done(((f32[32,2,64,128]{3,2,1,0:T(8,128)}), f32[32,2,64,128]{3,2,1,0:T(8,128)}, u32[]{:S(2)}, u32[]{:S(2)}) %all-to-all-start.2) | async-done | bytes 2097184 | tf_op jit(solution)/shard_map/all_to_all | solution.py:246
  130.2 5.6 %all-to-all-start.4 = ((f32[32,1,64,128]{3,2,1,0:T(8,128)}), f32[32,1,64,128]{3,2,1,0:T(8,128)S(1)}, u32[]{:S(2)}, u32[]{:S(2)}) async-start(f32[32,1,64,128]{3,2,1,0:T(8,128)} %window.2), calls=%async_computation.4 | async-start | bytes 2097152 | tf_op jit(solution)/shard_map/all_to_all | solution.py:252
  135.8 8.8 %window.3 = f32[32,3,64,128]{3,2,1,0:T(8,128)} custom-call(f32[512,512]{1,0:T(8,128)} %fusion.2.x_ref, f32[512,512]{1,0:T(8,128)} %fusion.y_ref, f32[32,1,64,128]{3,2,1,0:T(8,128)} %all-to-all-done.1.refs_0_, f32[32,2,64,128]{3,2,1,0:T(8,128)} %all-to-all-done.2.refs_1_), custom_call_target="tpu_custom_call" | custom-call | flops 4831838208 | bytes 4194304 | tf_op jit(solution)/shard_map/window/pallas_call | solution.py:151
  144.6 17.3 %all-to-all-done.4.refs_1_ = f32[32,1,64,128]{3,2,1,0:T(8,128)S(1)} async-done(((f32[32,1,64,128]{3,2,1,0:T(8,128)}), f32[32,1,64,128]{3,2,1,0:T(8,128)S(1)}, u32[]{:S(2)}, u32[]{:S(2)}) %all-to-all-start.4) | async-done | bytes 1048608 | tf_op jit(solution)/shard_map/all_to_all | solution.py:252
  161.9 1.0 copy-done.3
  162.8 4.2 %all-to-all-start.3 = ((f32[32,3,64,128]{3,2,1,0:T(8,128)}), f32[32,3,64,128]{3,2,1,0:T(8,128)S(1)}, u32[]{:S(2)}, u32[]{:S(2)}) async-start(f32[32,3,64,128]{3,2,1,0:T(8,128)} %window.3), calls=%async_computation.3 | async-start | bytes 6291456 | tf_op jit(solution)/shard_map/all_to_all | solution.py:252
  167.0 79.3 %psum.7 = f32[8]{0:T(128)S(1)} all-reduce(f32[8]{0:T(128)S(1)} %broadcast_multiply_fusion.1), channel_id=1, replica_groups=mesh['gx'=4,'gy'=8] {'gy'}, use_global_device_ids=true, to_apply=%region_3.4 | all-reduce | flops 8 | bytes 64 | tf_op jit(solution)/shard_map/psum | solution.py:254
  246.3 0.6 fusion.6
  246.9 0.0 all-to-all-done.3.refs_0_
  246.9 1.2 copy-done.4
  248.1 3.9 %restore.3 = f32[128,64,128]{2,1,0:T(8,128)} custom-call(f32[32,3,64,128]{3,2,1,0:T(8,128)S(1)} %all-to-all-done.3.refs_0_, f32[32,1,64,128]{3,2,1,0:T(8,128)S(1)} %copy-done.4), custom_call_target="tpu_custom_call" | custom-call | flops 1073741824 | bytes 8388608 | tf_op jit(solution)/shard_map/restore/pallas_call | solution.py:187
  (11 shorter events, 0.0 us)
Async XLA Ops:
  14.9 32.1 %all-to-all-start = ((f32[32,1,64,128]{3,2,1,0:T(8,128)}), f32[32,1,64,128]{3,2,1,0:T(8,128)S(1)}, u32[]{:S(2)}, u32[]{:S(2)}) async-start(f32[32,1,64,128]{3,2,1,0:T(8,128)} %get-tuple-element.13.refs_2_), calls=%async_computation | async-start | bytes 2097152 | tf_op jit(solution)/shard_map/all_to_all | solution.py:246
  47.0 4.7 %copy-start.6 = (f32[32,1,64,128]{3,2,1,0:T(8,128)}, f32[32,1,64,128]{3,2,1,0:T(8,128)S(1)}, u32[]{:S(2)}) copy-start(f32[32,1,64,128]{3,2,1,0:T(8,128)S(1)} %all-to-all-done.refs_0_) | copy-start | bytes 3145732
  47.0 30.8 %all-to-all-start.1 = ((f32[32,1,64,128]{3,2,1,0:T(8,128)}), f32[32,1,64,128]{3,2,1,0:T(8,128)}, u32[]{:S(2)}, u32[]{:S(2)}) async-start(f32[32,1,64,128]{3,2,1,0:T(8,128)} %get-tuple-element.14.refs_0_), calls=%async_computation.1 | async-start | bytes 2097152 | tf_op jit(solution)/shard_map/all_to_all | solution.py:246
  77.0 6.1 %copy-start.11 = (f32[512]{0:T(512)S(1)}, f32[512]{0:T(512)}, u32[]{:S(2)}) copy-start(f32[512]{0:T(512)} %param.14) | copy-start | bytes 6148
  77.0 6.2 %copy-start.10 = (f32[512]{0:T(512)S(1)}, f32[512]{0:T(512)}, u32[]{:S(2)}) copy-start(f32[512]{0:T(512)} %param.15) | copy-start | bytes 6148
  77.0 6.2 %copy-start.7 = (f32[2,2,8,128]{3,2,1,0:T(8,128)S(1)}, f32[2,2,8,128]{3,2,1,0:T(8,128)}, u32[]{:S(2)}) copy-start(f32[2,2,8,128]{3,2,1,0:T(8,128)} %get-tuple-element.19) | copy-start | bytes 49156
  77.1 6.2 %copy-start.8 = (f32[2,1,8,128]{3,2,1,0:T(8,128)S(1)}, f32[2,1,8,128]{3,2,1,0:T(8,128)}, u32[]{:S(2)}) copy-start(f32[2,1,8,128]{3,2,1,0:T(8,128)} %get-tuple-element.20) | copy-start | bytes 24580
  77.1 6.2 %copy-start.9 = (f32[2,1,8,128]{3,2,1,0:T(8,128)S(1)}, f32[2,1,8,128]{3,2,1,0:T(8,128)}, u32[]{:S(2)}) copy-start(f32[2,1,8,128]{3,2,1,0:T(8,128)} %get-tuple-element.18) | copy-start | bytes 24580
  77.1 6.3 %copy-start.12 = (s32[4,2,4]{2,1,0:T(2,128)S(1)}, s32[4,2,4]{2,1,0:T(2,128)}, u32[]{:S(2)}) copy-start(s32[4,2,4]{2,1,0:T(2,128)} %param.13) | copy-start | bytes 388
  77.1 6.5 %copy-start = (f32[32,2,64,128]{3,2,1,0:T(8,128)S(1)}, f32[32,2,64,128]{3,2,1,0:T(8,128)}, u32[]{:S(2)}) copy-start(f32[32,2,64,128]{3,2,1,0:T(8,128)} %get-tuple-element.15.refs_1_) | copy-start | bytes 6291460
  77.1 6.5 %copy-start.1 = (f32[32,1,64,128]{3,2,1,0:T(8,128)S(1)}, f32[32,1,64,128]{3,2,1,0:T(8,128)}, u32[]{:S(2)}) copy-start(f32[32,1,64,128]{3,2,1,0:T(8,128)} %get-tuple-element.13.refs_2_) | copy-start | bytes 3145732
  77.8 52.4 %all-to-all-start.2 = ((f32[32,2,64,128]{3,2,1,0:T(8,128)}), f32[32,2,64,128]{3,2,1,0:T(8,128)}, u32[]{:S(2)}, u32[]{:S(2)}) async-start(f32[32,2,64,128]{3,2,1,0:T(8,128)} %get-tuple-element.15.refs_1_), calls=%async_computation.2 | async-start | bytes 4194304 | tf_op jit(solution)/shard_map/all_to_all | solution.py:246
  83.6 1.2 copy-start.2
  84.8 4.4 %copy-start.13 = (f32[512]{0:T(512)S(1)}, f32[512]{0:T(512)}, u32[]{:S(2)}) copy-start(f32[512]{0:T(512)} %constant.17.clone) | copy-start | bytes 6148
  84.8 4.5 %copy-start.5 = (f32[512,512]{1,0:T(8,128)S(1)}, f32[512,512]{1,0:T(8,128)}, u32[]{:S(2)}) copy-start(f32[512,512]{1,0:T(8,128)} %constant.16.clone) | copy-start | bytes 3145732
  130.2 31.6 %all-to-all-start.4 = ((f32[32,1,64,128]{3,2,1,0:T(8,128)}), f32[32,1,64,128]{3,2,1,0:T(8,128)S(1)}, u32[]{:S(2)}, u32[]{:S(2)}) async-start(f32[32,1,64,128]{3,2,1,0:T(8,128)} %window.2), calls=%async_computation.4 | async-start | bytes 2097152 | tf_op jit(solution)/shard_map/all_to_all | solution.py:252
  161.9 1.0 copy-start.3
  162.8 84.1 %all-to-all-start.3 = ((f32[32,3,64,128]{3,2,1,0:T(8,128)}), f32[32,3,64,128]{3,2,1,0:T(8,128)S(1)}, u32[]{:S(2)}, u32[]{:S(2)}) async-start(f32[32,3,64,128]{3,2,1,0:T(8,128)} %window.3), calls=%async_computation.3 | async-start | bytes 6291456 | tf_op jit(solution)/shard_map/all_to_all | solution.py:252
  246.9 1.2 copy-start.4

commit v4 on v3

--- a/solution.py
+++ b/solution.py
@@ -193,7 +193,7 @@
         out_specs=pl.BlockSpec((size_x, ROWS, size_z), lambda j: (0, j, 0)),
         out_shape=jax.ShapeDtypeStruct((size_x, size_y, size_z), jnp.float32),
         cost_estimate=pl.CostEstimate(flops=1 << 30, bytes_accessed=8 << 20, transcendentals=0),
-        compiler_params=pltpu.CompilerParams(vmem_limit_bytes=16 << 20),
+        compiler_params=pltpu.CompilerParams(vmem_limit_bytes=54_000_000),
         name="restore",
     )(*parts)
 

time: 253 us -> 253 us (level)
  local copies, waits for them, and re-layouts: 3.79 us -> 0.39 us
  Pallas kernels: 75.1 us -> 78.1 us
    unnamed x28 -> x22, local copies, waits for them, and re-layouts: 3.46 us -> 0.06 us
    pallas_call x2, Pallas kernels: 8.17 us -> 11.2 us  [restore(): pl.pallas_call(functools.partial(restore_kernel, edge, len(parts)), grid=...]
where the time goes in v4:
time: 253 us; the launch traced here: 252 us
  blocking collectives  79.2 us (31%)
  Pallas kernels  78.1 us (31%)
  waiting for transfers between devices  60.4 us (24%)
  starting transfers between devices  26.5 us (10%)
  matrix products  5.7 us (2%)
    psum x1, blocking collectives, on_device(): lax.psum(contribution, 'gy')  79.2 us
    pallas_call x3, Pallas kernels, evaluate(): pl.pallas_call(functools.partial(evaluate_kernel, run_first, runs, edge,...  53.5 us
    all_to_all x3, waiting for transfers between devices, on_device(): pencils = [exchange(part) for part in cells]  43.1 us
    all_to_all x2, waiting for transfers between devices, on_device(): returned = [exchange(part) for part in filtered]  17.3 us
    all_to_all x3, starting transfers between devices, on_device(): pencils = [exchange(part) for part in cells]  16.1 us
    pallas_call x2, Pallas kernels, apply_window(): pl.pallas_call(functools.partial(window_kernel, span_x, span_y, first_pla...  13.5 us
    pallas_call x2, Pallas kernels, restore(): pl.pallas_call(functools.partial(restore_kernel, edge, len(parts)), grid=...  11.2 us
    all_to_all x2, starting transfers between devices, on_device(): returned = [exchange(part) for part in filtered]  10.4 us
  transfers between devices with their start and end apart: 5, of which 4 were waited for; matrix products, arithmetic and copies ran while one was open for 3% of the time, Pallas kernels for 23%

profile of v4, /device:TPU:8, one launch (start us, length us, event | category | flops | bytes accessed | tf_op | source)
XLA Modules:
  0.0 252.0 jit_solution(17275447896667007917)
XLA Ops:
  0.6 14.3 %evaluate.3 = (f32[32,1,64,128]{3,2,1,0:T(8,128)}, f32[2,1,8,128]{3,2,1,0:T(8,128)}) custom-call(s32[4,2,4]{2,1,0:T(2,128)} %mask_ref.5, f32[128,64,128]{2,1,0:T(8,128)} %field_ref.5, s32[64,4,128]{2,1,0:T(4,128)} %bitcast.8, bf16[64,128]{1,0:T(8,128)(2,1)} %bitcast.11), custom_call_target="tpu_custom_call" | custom-call | flops 67108864 | bytes 6291456 | tf_op jit(solution)/shard_map/evaluate/pallas_call | solution.py:81
  14.9 6.1 %all-to-all-start = ((f32[32,1,64,128]{3,2,1,0:T(8,128)}), f32[32,1,64,128]{3,2,1,0:T(8,128)S(1)}, u32[]{:S(2)}, u32[]{:S(2)}) async-start(f32[32,1,64,128]{3,2,1,0:T(8,128)} %get-tuple-element.13.refs_2_), calls=%async_computation | async-start | bytes 2097152 | tf_op jit(solution)/shard_map/all_to_all | solution.py:246
  21.0 13.9 %evaluate.4 = (f32[32,1,64,128]{3,2,1,0:T(8,128)}, f32[2,1,8,128]{3,2,1,0:T(8,128)}) custom-call(s32[4,2,4]{2,1,0:T(2,128)} %mask_ref.5, f32[128,64,128]{2,1,0:T(8,128)} %field_ref.5, s32[64,4,128]{2,1,0:T(4,128)} %bitcast.9, bf16[64,128]{1,0:T(8,128)(2,1)} %bitcast.12), custom_call_target="tpu_custom_call" | custom-call | flops 67108864 | bytes 6291456 | tf_op jit(solution)/shard_map/evaluate/pallas_call | solution.py:81
  34.8 12.1 %all-to-all-done.refs_0_ = f32[32,1,64,128]{3,2,1,0:T(8,128)S(1)} async-done(((f32[32,1,64,128]{3,2,1,0:T(8,128)}), f32[32,1,64,128]{3,2,1,0:T(8,128)S(1)}, u32[]{:S(2)}, u32[]{:S(2)}) %all-to-all-start) | async-done | bytes 1048608 | tf_op jit(solution)/shard_map/all_to_all | solution.py:246
  47.0 4.7 %all-to-all-start.1 = ((f32[32,1,64,128]{3,2,1,0:T(8,128)}), f32[32,1,64,128]{3,2,1,0:T(8,128)}, u32[]{:S(2)}, u32[]{:S(2)}) async-start(f32[32,1,64,128]{3,2,1,0:T(8,128)} %get-tuple-element.14.refs_0_), calls=%async_computation.1 | async-start | bytes 2097152 | tf_op jit(solution)/shard_map/all_to_all | solution.py:246
  51.7 25.3 %evaluate.5 = (f32[32,2,64,128]{3,2,1,0:T(8,128)}, f32[2,2,8,128]{3,2,1,0:T(8,128)}) custom-call(s32[4,2,4]{2,1,0:T(2,128)} %mask_ref.5, f32[128,64,128]{2,1,0:T(8,128)} %field_ref.5, s32[64,4,128]{2,1,0:T(4,128)} %bitcast.10, bf16[64,128]{1,0:T(8,128)(2,1)} %bitcast.13), custom_call_target="tpu_custom_call" | custom-call | flops 134217728 | bytes 6291456 | tf_op jit(solution)/shard_map/evaluate/pallas_call | solution.py:81
  77.0 0.0 copy-done.3
  77.0 0.0 copy-start.8
  77.0 0.0 copy-start.7
  77.0 0.0 copy-start.4
  77.1 0.0 copy-start.5
  77.1 0.0 copy-start.6
  77.1 0.0 copy-start.9
  77.1 0.0 copy-start
  77.1 0.0 copy-start.1
  77.1 0.7 all-to-all-done.1.refs_0_
  77.8 5.3 %all-to-all-start.2 = ((f32[32,2,64,128]{3,2,1,0:T(8,128)}), f32[32,2,64,128]{3,2,1,0:T(8,128)}, u32[]{:S(2)}, u32[]{:S(2)}) async-start(f32[32,2,64,128]{3,2,1,0:T(8,128)} %get-tuple-element.15.refs_1_), calls=%async_computation.2 | async-start | bytes 4194304 | tf_op jit(solution)/shard_map/all_to_all | solution.py:246
  83.1 0.0 copy-done.8
  83.1 0.1 slice.13
  83.2 0.0 copy-done.7
  83.2 0.1 slice.15
  83.3 0.0 copy-done.4
  83.3 0.0 copy-done.5
  83.3 0.0 copy-done.6
  83.3 0.1 reshape.18
  83.4 0.0 copy-done.9
  83.4 0.1 copy.13
  83.5 0.1 reduce_sum.37
  83.6 0.0 copy-done
  83.6 0.0 copy-done.1
  83.6 0.0 copy-start.10
  83.6 0.0 copy-start.2
  83.6 5.8 %restore.2 = f32[128,64,128]{2,1,0:T(8,128)} custom-call(f32[32,1,64,128]{3,2,1,0:T(8,128)S(1)} %copy-done.1, f32[32,2,64,128]{3,2,1,0:T(8,128)} %get-tuple-element.15.refs_1_, f32[32,1,64,128]{3,2,1,0:T(8,128)S(1)} %copy-done), custom_call_target="tpu_custom_call" | custom-call | flops 1073741824 | bytes 8388608 | tf_op jit(solution)/shard_map/restore/pallas_call | solution.py:187
  89.4 0.1 select_reduce_fusion
  89.5 0.1 maximum_multiply_fusion.1
  89.6 0.0 copy-done.2
  89.6 2.9 %fusion.y_ref = f32[512,512]{1,0:T(8,128)} fusion(f32[512,512]{1,0:T(8,128)S(1)} %copy-done.2, f32[512]{0:T(512)S(1)} %get-tuple-element.23), kind=kOutput, calls=%fused_computation | convolution fusion | flops 1610874880 | bytes 2099200 | tf_op jit(solution)/shard_map/dot_general | solution.py:214
  92.4 2.8 %fusion.2.x_ref = f32[512,512]{1,0:T(8,128)} fusion(f32[512,512]{1,0:T(8,128)S(1)} %copy-done.2, f32[512]{0:T(512)S(1)} %get-tuple-element.24), kind=kOutput, calls=%fused_computation.2 | convolution fusion | flops 1610874880 | bytes 2099200 | tf_op jit(solution)/shard_map/dot_general | solution.py:214
  95.3 4.7 %window.2 = f32[32,1,64,128]{3,2,1,0:T(8,128)} custom-call(f32[512,512]{1,0:T(8,128)} %fusion.2.x_ref, f32[512,512]{1,0:T(8,128)} %fusion.y_ref, f32[32,1,64,128]{3,2,1,0:T(8,128)} %copy-done.3), custom_call_target="tpu_custom_call" | custom-call | flops 1610612736 | bytes 4194304 | tf_op jit(solution)/shard_map/window/pallas_call | solution.py:151
  99.9 30.3 %all-to-all-done.2.refs_1_ = f32[32,2,64,128]{3,2,1,0:T(8,128)} async-done(((f32[32,2,64,128]{3,2,1,0:T(8,128)}), f32[32,2,64,128]{3,2,1,0:T(8,128)}, u32[]{:S(2)}, u32[]{:S(2)}) %all-to-all-start.2) | async-done | bytes 2097184 | tf_op jit(solution)/shard_map/all_to_all | solution.py:246
  130.2 5.6 %all-to-all-start.4 = ((f32[32,1,64,128]{3,2,1,0:T(8,128)}), f32[32,1,64,128]{3,2,1,0:T(8,128)S(1)}, u32[]{:S(2)}, u32[]{:S(2)}) async-start(f32[32,1,64,128]{3,2,1,0:T(8,128)} %window.2), calls=%async_computation.4 | async-start | bytes 2097152 | tf_op jit(solution)/shard_map/all_to_all | solution.py:252
  135.8 8.8 %window.3 = f32[32,3,64,128]{3,2,1,0:T(8,128)} custom-call(f32[512,512]{1,0:T(8,128)} %fusion.2.x_ref, f32[512,512]{1,0:T(8,128)} %fusion.y_ref, f32[32,1,64,128]{3,2,1,0:T(8,128)} %all-to-all-done.1.refs_0_, f32[32,2,64,128]{3,2,1,0:T(8,128)} %all-to-all-done.2.refs_1_), custom_call_target="tpu_custom_call" | custom-call | flops 4831838208 | bytes 4194304 | tf_op jit(solution)/shard_map/window/pallas_call | solution.py:151
  144.6 17.3 %all-to-all-done.4.refs_1_ = f32[32,1,64,128]{3,2,1,0:T(8,128)S(1)} async-done(((f32[32,1,64,128]{3,2,1,0:T(8,128)}), f32[32,1,64,128]{3,2,1,0:T(8,128)S(1)}, u32[]{:S(2)}, u32[]{:S(2)}) %all-to-all-start.4) | async-done | bytes 1048608 | tf_op jit(solution)/shard_map/all_to_all | solution.py:252
  161.9 4.9 %all-to-all-start.3 = ((f32[32,3,64,128]{3,2,1,0:T(8,128)}), f32[32,3,64,128]{3,2,1,0:T(8,128)}, u32[]{:S(2)}, u32[]{:S(2)}) async-start(f32[32,3,64,128]{3,2,1,0:T(8,128)} %window.3), calls=%async_computation.3 | async-start | bytes 6291456 | tf_op jit(solution)/shard_map/all_to_all | solution.py:252
  166.7 79.2 %psum.7 = f32[8]{0:T(128)S(1)} all-reduce(f32[8]{0:T(128)S(1)} %broadcast_multiply_fusion.1), channel_id=1, replica_groups=mesh['gx'=4,'gy'=8] {'gy'}, use_global_device_ids=true, to_apply=%region_3.4 | all-reduce | flops 8 | bytes 64 | tf_op jit(solution)/shard_map/psum | solution.py:254
  246.0 0.6 fusion.6
  246.6 0.0 all-to-all-done.3.refs_0_
  246.6 5.4 %restore.3 = f32[128,64,128]{2,1,0:T(8,128)} custom-call(f32[32,3,64,128]{3,2,1,0:T(8,128)} %all-to-all-done.3.refs_0_, f32[32,1,64,128]{3,2,1,0:T(8,128)S(1)} %all-to-all-done.4.refs_1_), custom_call_target="tpu_custom_call" | custom-call | flops 1073741824 | bytes 8388608 | tf_op jit(solution)/shard_map/restore/pallas_call | solution.py:187
  (5 shorter events, 0.0 us)
Async XLA Ops:
  14.9 32.1 %all-to-all-start = ((f32[32,1,64,128]{3,2,1,0:T(8,128)}), f32[32,1,64,128]{3,2,1,0:T(8,128)S(1)}, u32[]{:S(2)}, u32[]{:S(2)}) async-start(f32[32,1,64,128]{3,2,1,0:T(8,128)} %get-tuple-element.13.refs_2_), calls=%async_computation | async-start | bytes 2097152 | tf_op jit(solution)/shard_map/all_to_all | solution.py:246
  47.0 30.1 %copy-start.3 = (f32[32,1,64,128]{3,2,1,0:T(8,128)}, f32[32,1,64,128]{3,2,1,0:T(8,128)S(1)}, u32[]{:S(2)}) copy-start(f32[32,1,64,128]{3,2,1,0:T(8,128)S(1)} %all-to-all-done.refs_0_) | copy-start | bytes 3145732
  47.0 30.8 %all-to-all-start.1 = ((f32[32,1,64,128]{3,2,1,0:T(8,128)}), f32[32,1,64,128]{3,2,1,0:T(8,128)}, u32[]{:S(2)}, u32[]{:S(2)}) async-start(f32[32,1,64,128]{3,2,1,0:T(8,128)} %get-tuple-element.14.refs_0_), calls=%async_computation.1 | async-start | bytes 2097152 | tf_op jit(solution)/shard_map/all_to_all | solution.py:246
  77.0 6.1 %copy-start.8 = (f32[512]{0:T(512)S(1)}, f32[512]{0:T(512)}, u32[]{:S(2)}) copy-start(f32[512]{0:T(512)} %param.14) | copy-start | bytes 6148
  77.0 6.2 %copy-start.7 = (f32[512]{0:T(512)S(1)}, f32[512]{0:T(512)}, u32[]{:S(2)}) copy-start(f32[512]{0:T(512)} %param.15) | copy-start | bytes 6148
  77.0 6.2 %copy-start.4 = (f32[2,2,8,128]{3,2,1,0:T(8,128)S(1)}, f32[2,2,8,128]{3,2,1,0:T(8,128)}, u32[]{:S(2)}) copy-start(f32[2,2,8,128]{3,2,1,0:T(8,128)} %get-tuple-element.19) | copy-start | bytes 49156
  77.1 6.2 %copy-start.5 = (f32[2,1,8,128]{3,2,1,0:T(8,128)S(1)}, f32[2,1,8,128]{3,2,1,0:T(8,128)}, u32[]{:S(2)}) copy-start(f32[2,1,8,128]{3,2,1,0:T(8,128)} %get-tuple-element.20) | copy-start | bytes 24580
  77.1 6.2 %copy-start.6 = (f32[2,1,8,128]{3,2,1,0:T(8,128)S(1)}, f32[2,1,8,128]{3,2,1,0:T(8,128)}, u32[]{:S(2)}) copy-start(f32[2,1,8,128]{3,2,1,0:T(8,128)} %get-tuple-element.18) | copy-start | bytes 24580
  77.1 6.3 %copy-start.9 = (s32[4,2,4]{2,1,0:T(2,128)S(1)}, s32[4,2,4]{2,1,0:T(2,128)}, u32[]{:S(2)}) copy-start(s32[4,2,4]{2,1,0:T(2,128)} %param.13) | copy-start | bytes 388
  77.1 6.5 %copy-start = (f32[32,1,64,128]{3,2,1,0:T(8,128)S(1)}, f32[32,1,64,128]{3,2,1,0:T(8,128)}, u32[]{:S(2)}) copy-start(f32[32,1,64,128]{3,2,1,0:T(8,128)} %get-tuple-element.13.refs_2_) | copy-start | bytes 3145732
  77.1 6.5 %copy-start.1 = (f32[32,1,64,128]{3,2,1,0:T(8,128)S(1)}, f32[32,1,64,128]{3,2,1,0:T(8,128)}, u32[]{:S(2)}) copy-start(f32[32,1,64,128]{3,2,1,0:T(8,128)} %get-tuple-element.14.refs_0_) | copy-start | bytes 3145732
  77.8 52.4 %all-to-all-start.2 = ((f32[32,2,64,128]{3,2,1,0:T(8,128)}), f32[32,2,64,128]{3,2,1,0:T(8,128)}, u32[]{:S(2)}, u32[]{:S(2)}) async-start(f32[32,2,64,128]{3,2,1,0:T(8,128)} %get-tuple-element.15.refs_1_), calls=%async_computation.2 | async-start | bytes 4194304 | tf_op jit(solution)/shard_map/all_to_all | solution.py:246
  83.6 5.9 %copy-start.10 = (f32[512]{0:T(512)S(1)}, f32[512]{0:T(512)}, u32[]{:S(2)}) copy-start(f32[512]{0:T(512)} %constant.17.clone) | copy-start | bytes 6148
  83.6 6.0 %copy-start.2 = (f32[512,512]{1,0:T(8,128)S(1)}, f32[512,512]{1,0:T(8,128)}, u32[]{:S(2)}) copy-start(f32[512,512]{1,0:T(8,128)} %constant.16.clone) | copy-start | bytes 3145732
  130.2 31.6 %all-to-all-start.4 = ((f32[32,1,64,128]{3,2,1,0:T(8,128)}), f32[32,1,64,128]{3,2,1,0:T(8,128)S(1)}, u32[]{:S(2)}, u32[]{:S(2)}) async-start(f32[32,1,64,128]{3,2,1,0:T(8,128)} %window.2), calls=%async_computation.4 | async-start | bytes 2097152 | tf_op jit(solution)/shard_map/all_to_all | solution.py:252
  161.9 84.7 %all-to-all-start.3 = ((f32[32,3,64,128]{3,2,1,0:T(8,128)}), f32[32,3,64,128]{3,2,1,0:T(8,128)}, u32[]{:S(2)}, u32[]{:S(2)}) async-start(f32[32,3,64,128]{3,2,1,0:T(8,128)} %window.3), calls=%async_computation.3 | async-start | bytes 6291456 | tf_op jit(solution)/shard_map/all_to_all | solution.py:252
